TPU v7x, 768 devices: a whole 4x8x12 slice. The times are simulated.
768 devices in a mesh: stream: 16 (over y_hi, x, core), cross: 48 (over z, y_lo).
Axes of the slice: x: 4, y: 8 (y_hi: 2, y_lo: 4; y = y_hi * 4 + y_lo), z: 12, core: 2. Of those that a mesh axis runs over, the one named last changes fastest.
Arguments:
- state_now: float32 [7, 8, 384, 2048], P(None, None, 'cross', 'stream'), as said below
- state_base: float32 [7, 8, 384, 2048], P(None, None, 'cross', 'stream'), as said below
- inflow: float32 [7, 8, 384, 3], P(None, None, 'cross'), as said below
Outputs:
- state_next: float32 [7, 8, 384, 2048], P(None, None, 'cross', 'stream')
Inputs may be any that keep to these rules, and one draw needn't show every extreme that they name: `state_now`: partial densities and volume fractions are positive, volume fractions below 1, and the pressure that each cell implies is positive. `state_base`: partial densities and volume fractions are positive, volume fractions below 1, and the pressure that each cell implies is positive. `inflow`: partial densities and volume fractions are positive, volume fractions below 1, and the pressure that each cell implies is positive.
All inputs are finite; a program needn't handle non-finite values.
Results may differ from a plain program's by a relative error of at most 0.0003.
Values sent between devices are 32-bit elements; how exact they have to be, the bound alone decides.
A program may use at most 32 MiB of HBM per device.

v0:
```python
import jax
import jax.numpy as jnp
from jax import lax
from jax.sharding import PartitionSpec as P

gas_gamma = 1.4
liquid_gamma = 4.4
liquid_stiff = 0.6
courant = 0.3
weno_epsilon = 1e-06


def sent_to_all(array, axis):
    copies = jnp.broadcast_to(array, (lax.axis_size(axis), *array.shape))
    return lax.all_to_all(copies, axis, split_axis=0, concat_axis=0, tiled=True)


def of_everyone(array, axis):
    return sent_to_all(array, axis).max(axis=0)


def with_halo(array, sides, width, wrap):
    for axis, dim in sides:
        size, length = (lax.axis_size(axis), array.shape[dim])
        up = [(i, (i + 1) % size) for i in range(size if wrap else size - 1)]
        down = [(j, i) for i, j in up]
        last = lax.slice_in_dim(array, length - width, length, axis=dim)
        first = lax.slice_in_dim(array, 0, width, axis=dim)
        before = lax.ppermute(last, axis, up)
        after = lax.ppermute(first, axis, down)
        array = jnp.concatenate([before, array, after], axis=dim)
    return array


def mixture(volume):
    stiff_gamma = volume / (gas_gamma - 1.0) + (1.0 - volume) / (liquid_gamma - 1.0)
    stiff_term = (1.0 - volume) * liquid_gamma * liquid_stiff / (liquid_gamma - 1.0)
    return (stiff_gamma, stiff_term)


def primitive(conserved):
    density = conserved[0] + conserved[1]
    vel_one = conserved[2] / density
    vel_two = conserved[3] / density
    vel_three = conserved[4] / density
    kinetic = 0.5 * (conserved[2] * vel_one + conserved[3] * vel_two + conserved[4] * vel_three)
    stiff_gamma, stiff_term = mixture(conserved[6])
    pressure = (conserved[5] - kinetic - stiff_term) / stiff_gamma
    return jnp.stack(
        [conserved[0], conserved[1], vel_one, vel_two, vel_three, pressure, conserved[6]]
    )


def sound(primitives):
    density = primitives[0] + primitives[1]
    stiff_gamma, stiff_term = mixture(primitives[6])
    return jnp.sqrt(((stiff_gamma + 1.0) * primitives[5] + stiff_term) / (stiff_gamma * density))


def max_speed(conserved):
    primitives = primitive(conserved)
    fastest = jnp.maximum(
        jnp.maximum(jnp.abs(primitives[2]), jnp.abs(primitives[3])), jnp.abs(primitives[4])
    )
    return jnp.max(fastest + sound(primitives))


def weno_face(far_left, near_left, centre, near_right, far_right):
    first_low = far_left - 2.0 * near_left + centre
    second_low = far_left - 4.0 * near_left + 3.0 * centre
    first_mid = near_left - 2.0 * centre + near_right
    second_mid = near_left - near_right
    first_high = centre - 2.0 * near_right + far_right
    second_high = 3.0 * centre - 4.0 * near_right + far_right
    smooth_low = weno_epsilon + 13.0 / 12.0 * first_low * first_low + 0.25 * second_low * second_low
    smooth_mid = weno_epsilon + 13.0 / 12.0 * first_mid * first_mid + 0.25 * second_mid * second_mid
    smooth_high = (
        weno_epsilon + 13.0 / 12.0 * first_high * first_high + 0.25 * second_high * second_high
    )
    weight_low = 0.1 / (smooth_low * smooth_low)
    weight_mid = 0.6 / (smooth_mid * smooth_mid)
    weight_high = 0.3 / (smooth_high * smooth_high)
    guess_low = (2.0 * far_left - 7.0 * near_left + 11.0 * centre) / 6.0
    guess_mid = (-near_left + 5.0 * centre + 2.0 * near_right) / 6.0
    guess_high = (2.0 * centre + 5.0 * near_right - far_right) / 6.0
    return (weight_low * guess_low + weight_mid * guess_mid + weight_high * guess_high) / (
        weight_low + weight_mid + weight_high
    )


def clamp_face(state, lower_cell, upper_cell):
    smaller = jnp.minimum(lower_cell, upper_cell)
    larger = jnp.maximum(lower_cell, upper_cell)
    limited = []
    for component in range(7):
        face_value = state[component]
        if component in (0, 1, 5):
            face_value = jnp.maximum(face_value, 0.5 * smaller[component])
        elif component == 6:
            face_value = jnp.clip(face_value, 0.5 * smaller[6], 1.0 - 0.5 * (1.0 - larger[6]))
        limited.append(face_value)
    return jnp.stack(limited)


def side_terms(primitives, normal):
    density = primitives[0] + primitives[1]
    stiff_gamma, stiff_term = mixture(primitives[6])
    velocity = [primitives[2], primitives[3], primitives[4]]
    energy = (
        stiff_gamma * primitives[5]
        + stiff_term
        + 0.5
        * density
        * (velocity[0] * velocity[0] + velocity[1] * velocity[1] + velocity[2] * velocity[2])
    )
    normal_vel = velocity[normal]
    amounts = jnp.stack(
        [
            primitives[0],
            primitives[1],
            density * velocity[0],
            density * velocity[1],
            density * velocity[2],
            energy,
            primitives[6],
        ]
    )
    momentum = []
    for component in range(3):
        moved = density * velocity[component] * normal_vel
        if component == normal:
            moved = moved + primitives[5]
        momentum.append(moved)
    transport = jnp.stack(
        [
            primitives[0] * normal_vel,
            primitives[1] * normal_vel,
            momentum[0],
            momentum[1],
            momentum[2],
            (energy + primitives[5]) * normal_vel,
            primitives[6] * normal_vel,
        ]
    )
    signal = jnp.abs(normal_vel) + sound(primitives)
    return (amounts, transport, normal_vel, signal)


def face_flux(left_state, right_state, normal):
    amount_left, transport_left, normal_left, signal_left = side_terms(left_state, normal)
    amount_right, transport_right, normal_right, signal_right = side_terms(right_state, normal)
    fastest = jnp.maximum(signal_left, signal_right)
    face_fluxes = 0.5 * (transport_left + transport_right) - 0.5 * fastest * (
        amount_right - amount_left
    )
    return (face_fluxes, 0.5 * (normal_left + normal_right))


def direction_sweep(padded, dimension, normal):
    primitives = primitive(padded)
    length = padded.shape[dimension] - 6
    pieces = [
        lax.slice_in_dim(primitives, offset, offset + length + 1, axis=dimension)
        for offset in range(6)
    ]
    left_state = clamp_face(
        weno_face(pieces[0], pieces[1], pieces[2], pieces[3], pieces[4]), pieces[2], pieces[3]
    )
    right_state = clamp_face(
        weno_face(pieces[5], pieces[4], pieces[3], pieces[2], pieces[1]), pieces[2], pieces[3]
    )
    face_fluxes, face_motion = face_flux(left_state, right_state, normal)
    change = lax.slice_in_dim(face_fluxes, 1, length + 1, axis=dimension) - lax.slice_in_dim(
        face_fluxes, 0, length, axis=dimension
    )
    spread = lax.slice_in_dim(face_motion, 1, length + 1, axis=dimension - 1) - lax.slice_in_dim(
        face_motion, 0, length, axis=dimension - 1
    )
    return (change, spread)


def tendency(stream_cells, cross_cells, span_cells, centre_cells):
    change_stream, spread_stream = direction_sweep(stream_cells, 3, 0)
    change_cross, spread_cross = direction_sweep(cross_cells, 2, 1)
    change_span, spread_span = direction_sweep(span_cells, 1, 2)
    total = -(change_stream + change_cross + change_span)
    source = centre_cells[6] * (spread_stream + spread_cross + spread_span)
    return jnp.concatenate([total[:6], (total[6] + source)[None]], axis=0)


def shards(state_now, state_base, inflow):
    fastest_here = max_speed(state_base)
    slab_fastest = of_everyone(fastest_here, "cross")
    fastest = of_everyone(slab_fastest, "stream")
    time_step = courant / fastest
    cross_cells = with_halo(state_now, (("cross", 2),), 3, True)
    stream_cells = with_halo(state_now, (("stream", 3),), 3, False)
    position = lax.axis_index("stream")
    final_index = lax.axis_size("stream") - 1
    last_cells = jnp.repeat(state_now[:, :, :, -1:], 3, axis=3)
    lower_rim = jnp.where(position == 0, inflow, stream_cells[:, :, :, :3])
    upper_rim = jnp.where(position == final_index, last_cells, stream_cells[:, :, :, -3:])
    stream_cells = jnp.concatenate([lower_rim, state_now, upper_rim], axis=3)
    span_cells = jnp.concatenate([state_now[:, -3:], state_now, state_now[:, :3]], axis=1)
    changes = tendency(stream_cells, cross_cells, span_cells, state_now)
    return state_base / 3.0 + 2.0 / 3.0 * (state_now + time_step * changes)


def solution(mesh):
    return jax.shard_map(
        shards,
        mesh=mesh,
        in_specs=(
            P(None, None, "cross", "stream"),
            P(None, None, "cross", "stream"),
            P(None, None, "cross", None),
        ),
        out_specs=P(None, None, "cross", "stream"),
        check_vma=False,
    )
```

profile of v0, /device:TPU:1, one launch (start us, length us, event | category | flops | bytes accessed | tf_op | source)
XLA Modules:
  0.0 74.5 jit_solution(4945306078549674032)
XLA Ops:
  0.0 1.0 %copy.29 = f32[7,8,8,128]{3,1,2,0:T(8,128)S(1)} copy(f32[7,8,8,128]{3,2,1,0:T(8,128)} %param.3) | data formatting | bytes 458752 | tf_op args[0]
  1.0 0.1 fusion.162
  1.1 0.0 copy-start.1
  1.1 12.5 %collective-permute-start.1 = (f32[7,8,8,3]{3,1,2,0:T(8,128)S(1)}, f32[7,8,8,3]{3,1,2,0:T(8,128)S(1)}, u32[]{:S(2)}, u32[]{:S(2)}) collective-permute-start(f32[7,8,8,3]{3,1,2,0:T(8,128)S(1)} %get-tuple-element.129), channel_id=1, source_target_pairs={{48,0},{96,48},{144,96},{192,144},{240,192},{288,240},{336,288},{3... | collective-permute-start | bytes 16136 | tf_op jit(solution)/shard_map/ppermute | solution.py:30
  13.6 1.9 %collective-permute-start = (f32[7,8,8,3]{3,1,2,0:T(8,128)S(1)}, f32[7,8,8,3]{3,1,2,0:T(8,128)S(1)}, u32[]{:S(2)}, u32[]{:S(2)}) collective-permute-start(f32[7,8,8,3]{3,1,2,0:T(8,128)S(1)} %get-tuple-element.128), channel_id=1, source_target_pairs={{0,48},{48,96},{96,144},{144,192},{192,240},{240,288},{288,336},{3... | collective-permute-start | bytes 16136 | tf_op jit(solution)/shard_map/ppermute | solution.py:29
  15.6 1.9 %collective-permute-start.2 = (f32[7,8,3,128]{3,1,2,0:T(8,128)S(1)}, f32[7,8,3,128]{3,1,2,0:T(8,128)S(1)}, u32[]{:S(2)}, u32[]{:S(2)}) collective-permute-start(f32[7,8,3,128]{3,1,2,0:T(8,128)S(1)} %get-tuple-element.131), channel_id=1, source_target_pairs={{0,1},{1,2},{2,3},{3,4},{4,5},{5,6},{6,7},{7,8},{8,9},{9,10},{10,1... | collective-permute-start | bytes 258056 | tf_op jit(solution)/shard_map/ppermute | solution.py:29
  17.5 9.5 %collective-permute-start.3 = (f32[7,8,3,128]{3,1,2,0:T(8,128)S(1)}, f32[7,8,3,128]{3,1,2,0:T(8,128)S(1)}, u32[]{:S(2)}, u32[]{:S(2)}) collective-permute-start(f32[7,8,3,128]{3,1,2,0:T(8,128)S(1)} %get-tuple-element.130), channel_id=1, source_target_pairs={{1,0},{2,1},{3,2},{4,3},{5,4},{6,5},{7,6},{8,7},{9,8},{10,9},{11,1... | collective-permute-start | bytes 258056 | tf_op jit(solution)/shard_map/ppermute | solution.py:30
  27.0 0.0 copy-done.1
  27.0 0.7 add_reduce_fusion
  27.7 1.3 %broadcast_in_dim.6 = f32[48,1,1]{2,1,0:T(1,128)} broadcast(f32[]{:T(128)} %add_reduce_fusion), dimensions={} | broadcast | bytes 196 | tf_op jit(solution)/shard_map/broadcast_in_dim | solution.py:14
  29.0 4.6 %all-to-all-start = ((f32[48,1,1]{2,1,0:T(1,128)}), f32[48,1,1]{2,1,0:T(1,128)S(1)}, u32[]{:S(2)}, u32[]{:S(2)}) async-start(f32[48,1,1]{2,1,0:T(1,128)} %broadcast_in_dim.6), calls=%async_computation | async-start | bytes 49152 | tf_op jit(solution)/shard_map/all_to_all | solution.py:15
  33.7 0.1 pad_maximum_fusion.1
  33.9 0.1 constant_dynamic-update-slice_fusion.72
  33.9 2.1 %fusion.160 = (f32[7,9,8,128]{3,1,2,0:T(8,128)S(1)}, f32[7,9,8,128]{3,1,2,0:T(8,128)S(1)}, f32[7,9,8,128]{3,1,2,0:T(8,128)S(1)}, f32[7,9,8,128]{3,1,2,0:T(8,128)S(1)}, f32[7,9,8,128]{3,1,2,0:T(8,128)S(1)}) fusion(f32[7,14,8,128]{3,1,2,0:T(8,128)S(1)} %constant_dynamic-update-slice_fusion.71), kind=kLoop, calls=%fused_computation.421 | loop fusion | flops 8064000 | bytes 2838528 | tf_op jit(solution)/shard_map/slice | solution.py:163
  36.1 0.2 multiply_bitcast_fusion.1
  36.5 0.1 constant_dynamic-update-slice_fusion.78
  36.6 0.0 copy-start
  36.7 0.1 multiply_subtract_fusion
  36.8 0.8 %copy-done = f32[7,8,8,128]{3,2,1,0:T(8,128)S(1)} copy-done((f32[7,8,8,128]{3,2,1,0:T(8,128)S(1)}, f32[7,8,8,128]{3,2,1,0:T(8,128)}, u32[]{:S(2)}) %copy-start) | copy-done | bytes 229400
  37.6 0.1 slice.435
  37.7 0.0 copy-start.2
  37.7 0.4 copy.34
  38.1 6.6 %all-to-all-done = f32[48,1,1]{2,1,0:T(1,128)S(1)} async-done(((f32[48,1,1]{2,1,0:T(1,128)}), f32[48,1,1]{2,1,0:T(1,128)S(1)}, u32[]{:S(2)}, u32[]{:S(2)}) %all-to-all-start) | async-done | bytes 224 | tf_op jit(solution)/shard_map/all_to_all | solution.py:15
  44.7 0.7 reduce_max.28
  45.5 1.3 %broadcast_in_dim.14 = f32[16,1,1]{2,1,0:T(1,128)} broadcast(f32[]{:T(128)} %reduce_max.28), dimensions={} | broadcast | bytes 68 | tf_op jit(solution)/shard_map/broadcast_in_dim | solution.py:14
  46.7 10.6 %all-to-all-start.1 = ((f32[16,1,1]{2,1,0:T(1,128)}), f32[16,1,1]{2,1,0:T(1,128)S(1)}, u32[]{:S(2)}, u32[]{:S(2)}) async-start(f32[16,1,1]{2,1,0:T(1,128)} %broadcast_in_dim.14), calls=%async_computation.1 | async-start | bytes 16384 | tf_op jit(solution)/shard_map/all_to_all | solution.py:15
  57.3 0.0 copy-done.2
  57.3 0.4 copy.17
  57.7 8.9 %all-to-all-done.1 = f32[16,1,1]{2,1,0:T(1,128)S(1)} async-done(((f32[16,1,1]{2,1,0:T(1,128)}), f32[16,1,1]{2,1,0:T(1,128)S(1)}, u32[]{:S(2)}, u32[]{:S(2)}) %all-to-all-start.1) | async-done | bytes 96 | tf_op jit(solution)/shard_map/all_to_all | solution.py:15
  66.7 0.6 reduce_max.29
  68.0 0.0 collective-permute-done.1
  68.0 0.1 broadcast_select_fusion
  68.1 0.0 collective-permute-done
  68.2 0.2 pad_maximum_fusion
  68.5 0.1 constant_dynamic-update-slice_fusion.1
  68.6 2.2 %fusion.159 = (f32[7,8,8,129]{3,1,2,0:T(8,128)S(1)}, f32[7,8,8,129]{3,1,2,0:T(8,128)S(1)}, f32[7,8,8,129]{3,1,2,0:T(8,128)S(1)}, f32[7,8,8,129]{3,1,2,0:T(8,128)S(1)}, f32[7,8,8,129]{3,1,2,0:T(8,128)S(1)}) fusion(f32[7,8,8,134]{3,1,2,0:T(8,128)S(1)} %constant_dynamic-update-slice_fusion), kind=kLoop, calls=%fused_computation.420 | loop fusion | flops 7224000 | bytes 2542848 | tf_op jit(solution)/shard_map/slice | solution.py:163
  70.8 0.2 multiply_bitcast_fusion.2
  71.2 0.1 constant_dynamic-update-slice_fusion.7
  71.4 0.1 multiply_subtract_fusion.3
  71.5 0.0 collective-permute-done.2
  71.6 0.0 collective-permute-done.3
  71.8 1.1 %fusion.161 = (f32[7,8,9,128]{3,1,2,0:T(8,128)S(1)}, f32[7,8,9,128]{3,1,2,0:T(8,128)S(1)}, f32[7,8,9,128]{3,1,2,0:T(8,128)S(1)}, f32[7,8,9,128]{3,1,2,0:T(8,128)S(1)}, f32[7,8,9,128]{3,1,2,0:T(8,128)S(1)}) fusion(f32[7,8,14,128]{3,1,2,0:T(8,128)S(1)} %constant_dynamic-update-slice_fusion.37), kind=kLoop, calls=%fused_computation.422 | loop fusion | flops 8064000 | bytes 2838528 | tf_op jit(solution)/shard_map/slice | solution.py:163
  72.9 0.1 multiply_bitcast_fusion.4
  73.1 0.1 constant_dynamic-update-slice_fusion.44
  73.3 0.1 multiply_subtract_fusion.6
  73.4 0.1 fusion.103
  73.5 0.1 fusion.133
  73.6 0.1 fusion.107
  73.7 0.7 copy.30
  (57 shorter events, 1.1 us)
Async XLA Ops:
  1.1 25.9 %copy-start.1 = (f32[7,8,8,128]{3,2,1,0:T(8,128)S(1)}, f32[7,8,8,128]{3,2,1,0:T(8,128)}, u32[]{:S(2)}) copy-start(f32[7,8,8,128]{3,2,1,0:T(8,128)} %param.4) | copy-start | bytes 688132
  1.1 66.9 %collective-permute-start.1 = (f32[7,8,8,3]{3,1,2,0:T(8,128)S(1)}, f32[7,8,8,3]{3,1,2,0:T(8,128)S(1)}, u32[]{:S(2)}, u32[]{:S(2)}) collective-permute-start(f32[7,8,8,3]{3,1,2,0:T(8,128)S(1)} %get-tuple-element.129), channel_id=1, source_target_pairs={{48,0},{96,48},{144,96},{192,144},{240,192},{288,240},{336,288},{3... | collective-permute-start | bytes 16136 | tf_op jit(solution)/shard_map/ppermute | solution.py:30
  13.6 54.5 %collective-permute-start = (f32[7,8,8,3]{3,1,2,0:T(8,128)S(1)}, f32[7,8,8,3]{3,1,2,0:T(8,128)S(1)}, u32[]{:S(2)}, u32[]{:S(2)}) collective-permute-start(f32[7,8,8,3]{3,1,2,0:T(8,128)S(1)} %get-tuple-element.128), channel_id=1, source_target_pairs={{0,48},{48,96},{96,144},{144,192},{192,240},{240,288},{288,336},{3... | collective-permute-start | bytes 16136 | tf_op jit(solution)/shard_map/ppermute | solution.py:29
  15.6 55.9 %collective-permute-start.2 = (f32[7,8,3,128]{3,1,2,0:T(8,128)S(1)}, f32[7,8,3,128]{3,1,2,0:T(8,128)S(1)}, u32[]{:S(2)}, u32[]{:S(2)}) collective-permute-start(f32[7,8,3,128]{3,1,2,0:T(8,128)S(1)} %get-tuple-element.131), channel_id=1, source_target_pairs={{0,1},{1,2},{2,3},{3,4},{4,5},{5,6},{6,7},{7,8},{8,9},{9,10},{10,1... | collective-permute-start | bytes 258056 | tf_op jit(solution)/shard_map/ppermute | solution.py:29
  17.5 54.1 %collective-permute-start.3 = (f32[7,8,3,128]{3,1,2,0:T(8,128)S(1)}, f32[7,8,3,128]{3,1,2,0:T(8,128)S(1)}, u32[]{:S(2)}, u32[]{:S(2)}) collective-permute-start(f32[7,8,3,128]{3,1,2,0:T(8,128)S(1)} %get-tuple-element.130), channel_id=1, source_target_pairs={{1,0},{2,1},{3,2},{4,3},{5,4},{6,5},{7,6},{8,7},{9,8},{10,9},{11,1... | collective-permute-start | bytes 258056 | tf_op jit(solution)/shard_map/ppermute | solution.py:30
  29.0 15.7 %all-to-all-start = ((f32[48,1,1]{2,1,0:T(1,128)}), f32[48,1,1]{2,1,0:T(1,128)S(1)}, u32[]{:S(2)}, u32[]{:S(2)}) async-start(f32[48,1,1]{2,1,0:T(1,128)} %broadcast_in_dim.6), calls=%async_computation | async-start | bytes 49152 | tf_op jit(solution)/shard_map/all_to_all | solution.py:15
  36.6 0.9 %copy-start = (f32[7,8,8,128]{3,2,1,0:T(8,128)S(1)}, f32[7,8,8,128]{3,2,1,0:T(8,128)}, u32[]{:S(2)}) copy-start(f32[7,8,8,128]{3,2,1,0:T(8,128)} %param.3) | copy-start | bytes 688132
  37.7 19.6 %copy-start.2 = (f32[7,8,8,3]{2,1,3,0:T(8,128)S(1)}, f32[7,8,8,3]{2,1,3,0:T(8,128)}, u32[]{:S(2)}) copy-start(f32[7,8,8,3]{2,1,3,0:T(8,128)} %param.5) | copy-start | bytes 16132
  46.7 19.9 %all-to-all-start.1 = ((f32[16,1,1]{2,1,0:T(1,128)}), f32[16,1,1]{2,1,0:T(1,128)S(1)}, u32[]{:S(2)}, u32[]{:S(2)}) async-start(f32[16,1,1]{2,1,0:T(1,128)} %broadcast_in_dim.14), calls=%async_computation.1 | async-start | bytes 16384 | tf_op jit(solution)/shard_map/all_to_all | solution.py:15
where the time goes:
time: 74.8 us; the launch traced here: 74.5 us
  starting transfers between devices  41 us (55%)
  waiting for transfers between devices  15.6 us (21%)
  other arithmetic  10.3 us (14%)
  local copies, waits for them, and re-layouts  6.37 us (9%)
  between operations  1.3 us (2%)
    ppermute x2, starting transfers between devices, with_halo(): after = lax.ppermute(first, axis, down)  22 us
    all_to_all x2, waiting for transfers between devices, sent_to_all(): return lax.all_to_all(copies, axis, split_axis=0, concat_axis=0, tiled=True)  15.5 us
    all_to_all x2, starting transfers between devices, sent_to_all(): return lax.all_to_all(copies, axis, split_axis=0, concat_axis=0, tiled=True)  15.2 us
    slice x3, other arithmetic, direction_sweep(): lax.slice_in_dim(primitives, offset, offset + length + 1, axis=dimension)  5.45 us
    ppermute x2, starting transfers between devices, with_halo(): before = lax.ppermute(last, axis, up)  3.84 us
    broadcast_in_dim x2, local copies, waits for them, and re-layouts, sent_to_all(): copies = jnp.broadcast_to(array, (lax.axis_size(axis), *array.shape))  2.58 us
    unnamed x19, local copies, waits for them, and re-layouts  2.32 us
  transfers between devices with their start and end apart: 6, of which 2 were waited for; matrix products, arithmetic and copies ran while one was open for 16% of the time, Pallas kernels for 0%

commit v1 on v0

v1 whole, which is shorter than its diff:
```python
import functools

import jax
import jax.numpy as jnp
from jax import lax
from jax.experimental import pallas as pl
from jax.experimental.pallas import tpu as pltpu
from jax.sharding import PartitionSpec as P

MESH = pl.DeviceIdType.MESH

gas_part = 1.0 / 0.4
liquid_part = 1.0 / 3.4
stiff_part = 4.4 * 0.6 / 3.4


def inverse(value):
    guess = pl.reciprocal(value, approx=True)
    return guess * (2.0 - value * guess)


def mixture(volume):
    rest = 1.0 - volume
    return (volume * gas_part + rest * liquid_part, rest * stiff_part)


def primitive(u):
    over = 1.0 / (u[0] + u[1])
    vx, vy, vz = (u[2] * over, u[3] * over, u[4] * over)
    kinetic = 0.5 * (u[2] * vx + u[3] * vy + u[4] * vz)
    gamma, stiff = mixture(u[6])
    return (u[0], u[1], vx, vy, vz, (u[5] - kinetic - stiff) / gamma, u[6])


def sound(density, pressure, gamma, stiff):
    return jnp.sqrt(((gamma + 1.0) * pressure + stiff) / (gamma * density))


def edges(h, d1, d2, d3, d4):
    e1, e2, e3 = (d2 - d1, d3 - d2, d4 - d3)
    u0 = e1 + d2 + d2
    u1 = d2 + d3
    u2 = e3 - d3 - d3
    third = 13.0 / 3.0
    top = 1e30
    s0 = jnp.minimum(third * (e1 * e1) + u0 * u0 + 4e-6, top)
    s1 = jnp.minimum(third * (e2 * e2) + u1 * u1 + 4e-6, top)
    s2 = jnp.minimum(third * (e3 * e3) + u2 * u2 + 4e-6, top)
    r0, r1, r2 = (inverse(s0), inverse(s1), inverse(s2))
    a0, a1, a2 = (r0 * r0, 6.0 * (r1 * r1), r2 * r2)
    b0, b2 = (3.0 * a0, 3.0 * a2)
    up = a0 * (u0 + e1 + d2) + a1 * (u1 + d3) + b2 * (d3 - u2)
    down = a2 * (u2 + e3 - d3) - a1 * (u1 + d2) - b0 * (u0 + d2)
    upper = h + up * inverse(6.0 * (a0 + a1 + b2))
    lower = h + down * inverse(6.0 * (a2 + a1 + b0))
    return (upper, lower)


def limited(face, lower_cell, upper_cell):
    out = []
    for c in range(7):
        value = face[c]
        if c in (0, 1, 5):
            value = jnp.maximum(value, 0.5 * jnp.minimum(lower_cell[c], upper_cell[c]))
        elif c == 6:
            value = jnp.maximum(value, 0.5 * jnp.minimum(lower_cell[c], upper_cell[c]))
            value = jnp.minimum(value, 0.5 + 0.5 * jnp.maximum(lower_cell[c], upper_cell[c]))
        out.append(value)
    return out


def side(w, normal):
    density = w[0] + w[1]
    gamma, stiff = mixture(w[6])
    momentum = [density * w[2], density * w[3], density * w[4]]
    energy = (
        gamma * w[5]
        + stiff
        + 0.5 * (momentum[0] * w[2] + momentum[1] * w[3] + momentum[2] * w[4])
    )
    vn = w[2 + normal]
    amounts = [w[0], w[1], *momentum, energy, w[6]]
    moved = [amount * vn for amount in amounts]
    moved[2 + normal] = moved[2 + normal] + w[5]
    moved[5] = moved[5] + w[5] * vn
    signal = jnp.abs(vn) + sound(density, w[5], gamma, stiff)
    return (amounts, moved, vn, signal)


def fluxes(left, right, lower_cell, upper_cell, normal):
    one = side(limited(left, lower_cell, upper_cell), normal)
    two = side(limited(right, lower_cell, upper_cell), normal)
    fastest = jnp.maximum(one[3], two[3])
    out = [
        (fl + fr) - fastest * (ur - ul)
        for ul, ur, fl, fr in zip(one[0], two[0], one[1], two[1])
    ]
    return out + [one[2] + two[2]]


def rolled(value, shift, axis):
    return pltpu.roll(value, shift % value.shape[axis], axis)


def along(w, axis, normal):
    upper, lower, before = ([], [], [])
    for c in range(7):
        h = w[c]
        g = rolled(h, 1, axis)
        d2 = h - g
        d1, d3, d4 = (rolled(d2, 1, axis), rolled(d2, -1, axis), rolled(d2, -2, axis))
        up, down = edges(h, d1, d2, d3, d4)
        upper.append(rolled(up, 1, axis))
        lower.append(down)
        before.append(g)
    return fluxes(upper, lower, before, w, normal)


def spread(flux, axis, keep=None):
    if keep is not None:
        flux = [jnp.where(keep, f, 0.0) for f in flux]
    return [rolled(f, -1, axis) - f for f in flux]


def folded(change, volume):
    return change[:6] + [change[6] - volume * change[7]]


def ring(stage, sizes):
    inner_s, inner_c, outer_s, outer_c = sizes
    s, c = (lax.axis_index("stream"), lax.axis_index("cross"))
    if stage == 0:
        base = s // inner_s * inner_s
        return inner_s, lambda k: (base + (s - base + k) % inner_s, c)
    if stage == 1:
        n = outer_s * inner_c
        place = s // inner_s * inner_c + c % inner_c

        def at(k):
            there = (place + k) % n
            return (
                there // inner_c * inner_s + s % inner_s,
                c // inner_c * inner_c + there % inner_c,
            )

        return n, at
    return outer_c, lambda k: (s, (c + k * inner_c) % (outer_c * inner_c))


def send(source, target, send_sem, recv_sem, to):
    return pltpu.make_async_remote_copy(
        src_ref=source,
        dst_ref=target,
        send_sem=send_sem,
        recv_sem=recv_sem,
        device_id=to,
        device_id_type=MESH,
    )


def kernel(
    sizes,
    now_ref,
    base_ref,
    inflow_ref,
    rate_ref,
    fast_ref,
    cells,
    base,
    inflow,
    prim,
    xr,
    flux_prev,
    acc,
    a_own,
    a_left,
    a_right,
    edge,
    rows,
    slots0,
    slots1,
    slots2,
    in_sems,
    halo_send,
    halo_recv,
    stage_send,
    stage_recv,
):
    size_s, size_c = (sizes[0] * sizes[2], sizes[1] * sizes[3])
    s, c = (lax.axis_index("stream"), lax.axis_index("cross"))
    left, right = (((s + size_s - 1) % size_s, c), ((s + 1) % size_s, c))
    below, above = ((s, (c + size_c - 1) % size_c), (s, (c + 1) % size_c))
    slots = (slots0, slots1, slots2)
    stages = [ring(k, sizes) for k in range(3)]

    barrier = pltpu.get_barrier_semaphore()
    count = 0
    for stage in (2, 1, 0):
        n, at = stages[stage]
        for k in range(1, n):
            pl.semaphore_signal(barrier, inc=1, device_id=at(k), device_id_type=MESH)
            count += 1
    for there in (below, above, left, right):
        pl.semaphore_signal(barrier, inc=1, device_id=there, device_id_type=MESH)
        count += 1

    load_base = pltpu.make_async_copy(base_ref, base, in_sems.at[0])
    load_now = pltpu.make_async_copy(now_ref, cells.at[:, 3:11], in_sems.at[1])
    load_inflow = pltpu.make_async_copy(inflow_ref, inflow, in_sems.at[2])
    load_base.start()
    load_now.start()
    load_inflow.start()

    def all_of(ref, *index):
        return [ref[(k, *index)] for k in range(7)]

    def speed(y, most):
        w = primitive(all_of(base, y))
        gamma, stiff = mixture(w[6])
        swift = jnp.maximum(jnp.maximum(jnp.abs(w[2]), jnp.abs(w[3])), jnp.abs(w[4]))
        return jnp.maximum(most, swift + sound(w[0] + w[1], w[5], gamma, stiff))

    load_base.wait()
    most = lax.fori_loop(0, 8, speed, jnp.zeros((8, 128), jnp.float32))
    rows[0] = jnp.broadcast_to(jnp.max(most, keepdims=True), (1, 128))
    load_now.wait()
    load_inflow.wait()

    lane = lax.broadcasted_iota(jnp.int32, (8, 128), 1)
    place = lane % 16
    group = lane // 16
    for k in range(7):
        packed = rolled(cells[k, 3], 5, 1)
        for y in range(1, 8):
            packed = jnp.where(group == y, rolled(cells[k, 3 + y], 16 * y + 5, 1), packed)
        a_own[k] = packed

    def to_prim(y, _):
        for k, value in enumerate(primitive(all_of(cells, y))):
            prim[k, y] = value
        return 0

    pl.semaphore_wait(barrier, count)

    copies = [
        send(cells.at[:, 3:6], cells.at[:, 11:14], halo_send.at[0], halo_recv.at[0], below),
        send(cells.at[:, 8:11], cells.at[:, 0:3], halo_send.at[1], halo_recv.at[1], above),
        send(a_own, a_right, halo_send.at[2], halo_recv.at[2], left),
        send(a_own, a_left, halo_send.at[3], halo_recv.at[3], right),
    ]

    def stage_start(stage):
        n, at = stages[stage]
        for k in range(1, n):
            send(
                rows.at[stage],
                slots[stage].at[k - 1],
                stage_send.at[stage],
                stage_recv.at[stage],
                at(k),
            ).start()

    def stage_total(stage):
        n, at = stages[stage]
        return send(slots[stage], slots[stage], stage_send.at[stage], stage_recv.at[stage], at(1))

    def stage_end(stage):
        n, _ = stages[stage]
        stage_total(stage).wait_recv()
        value = rows[stage]
        for k in range(1, n):
            value = jnp.maximum(value, slots[stage][k - 1])
        return value

    stage_start(0)
    for copy in copies:
        copy.start()

    lax.fori_loop(3, 11, to_prim, 0)

    def local(y, _):
        w = all_of(prim, y + 3)
        across = folded(spread(along(w, 0, 2), 0), w[6])
        keep = (lane >= 3) & (lane <= 125)
        stream = folded(spread(along(w, 1, 0), 1, keep), w[6])
        for k in range(7):
            acc[k, y + 1] = across[k] + stream[k]
        return 0

    lax.fori_loop(0, 8, local, 0)

    rows[1] = stage_end(0)
    stage_start(1)

    for copy in copies:
        copy.wait_recv()

    @pl.when(s == 0)
    def _():
        for k in range(7):
            value = jnp.zeros((8, 128), jnp.float32)
            for layer in range(3):
                for y in range(8):
                    one = jnp.broadcast_to(inflow[k, layer][:, y : y + 1], (8, 128))
                    value = jnp.where((group == y) & (place == 2 + layer), one, value)
            a_left[k] = value

    @pl.when(s == size_s - 1)
    def _():
        for k in range(7):
            value = a_own[k]
            one, two, three = (rolled(value, 1, 1), rolled(value, 2, 1), rolled(value, 3, 1))
            a_right[k] = jnp.where(place == 5, one, jnp.where(place == 6, two, three))

    rim = []
    for k in range(7):
        own = a_own[k]
        late = rolled(jnp.where(place < 5, a_left[k], own), 6, 1)
        rim.append(jnp.where(place < 5, own, jnp.where(place < 8, a_right[k], late)))
    w = primitive(rim)
    keep = ((place >= 3) & (place <= 5)) | ((place >= 11) & (place <= 13))
    ends = folded(spread(along(w, 1, 0), 1, keep), w[6])
    for k in range(7):
        edge[k] = jnp.where(place < 5, ends[k], rolled(ends[k], -6, 1))

    lax.fori_loop(0, 3, to_prim, 0)
    lax.fori_loop(11, 14, to_prim, 0)

    def cell_edges(y):
        upper, lower = ([], [])
        for k in range(7):
            f, g, h, up, far = (prim[k, y + i] for i in range(1, 6))
            one, two = edges(h, g - f, h - g, up - h, far - up)
            upper.append(one)
            lower.append(two)
        return (upper, lower)

    for k, value in enumerate(cell_edges(-1 + 0)[0]):
        xr[k] = value
    for k in range(8):
        flux_prev[k] = jnp.zeros((8, 128), jnp.float32)
    for k in range(7):
        acc[k, 0] = jnp.zeros((8, 128), jnp.float32)

    def face(j, _):
        upper, lower = cell_edges(j)
        before = all_of(xr)
        for k in range(7):
            xr[k] = upper[k]
        lower_cell = all_of(prim, j + 2)
        flux = fluxes(before, lower, lower_cell, all_of(prim, j + 3), 1)
        change = [flux[k] - flux_prev[k] for k in range(8)]
        for k in range(8):
            flux_prev[k] = flux[k]
        for k, value in enumerate(folded(change, lower_cell[6])):
            acc[k, j] = acc[k, j] + value
        return 0

    lax.fori_loop(0, 9, face, 0)

    rows[2] = stage_end(1)
    stage_start(2)

    near = (lane >= 125) | (lane <= 2)
    for k in range(7):
        for y in range(8):
            extra = jnp.where(near, rolled(edge[k], 123 - 16 * y, 1), 0.0)
            rate_ref[k, y] = acc[k, y + 1] + extra

    fast_ref[...] = stage_end(2)
    for copy in copies:
        copy.wait_send()
    for stage in range(3):
        stage_total(stage).wait_send()


def shards(sizes, state_now, state_base, inflow):
    size = jnp.float32
    n0, n1, n2 = (sizes[0], sizes[1] * sizes[2], sizes[3])
    now_t = jnp.transpose(state_now, (0, 2, 1, 3))
    base_t = jnp.transpose(state_base, (0, 2, 1, 3))
    inflow_t = jnp.transpose(inflow, (0, 3, 1, 2))
    rate, fast = pl.pallas_call(
        functools.partial(kernel, sizes),
        out_shape=(
            jax.ShapeDtypeStruct((7, 8, 8, 128), size),
            jax.ShapeDtypeStruct((1, 128), size),
        ),
        in_specs=[pl.BlockSpec(memory_space=pl.ANY)] * 3,
        out_specs=(pl.BlockSpec(memory_space=pltpu.VMEM),) * 2,
        scratch_shapes=[
            pltpu.VMEM((7, 14, 8, 128), size),
            pltpu.VMEM((7, 8, 8, 128), size),
            pltpu.VMEM((7, 3, 8, 8), size),
            pltpu.VMEM((7, 14, 8, 128), size),
            pltpu.VMEM((7, 8, 128), size),
            pltpu.VMEM((8, 8, 128), size),
            pltpu.VMEM((7, 9, 8, 128), size),
            pltpu.VMEM((7, 8, 128), size),
            pltpu.VMEM((7, 8, 128), size),
            pltpu.VMEM((7, 8, 128), size),
            pltpu.VMEM((7, 8, 128), size),
            pltpu.VMEM((3, 1, 128), size),
            pltpu.VMEM((n0 - 1, 1, 128), size),
            pltpu.VMEM((n1 - 1, 1, 128), size),
            pltpu.VMEM((n2 - 1, 1, 128), size),
            pltpu.SemaphoreType.DMA((3,)),
            pltpu.SemaphoreType.DMA((4,)),
            pltpu.SemaphoreType.DMA((4,)),
            pltpu.SemaphoreType.DMA((3,)),
            pltpu.SemaphoreType.DMA((3,)),
        ],
        compiler_params=pltpu.CompilerParams(collective_id=0, has_side_effects=True),
    )(now_t, base_t, inflow_t)
    step = 0.3 / fast[0, 0]
    rate = jnp.transpose(rate, (0, 2, 1, 3)) * -0.5
    return state_base / 3.0 + 2.0 / 3.0 * (state_now + step * rate)


def solution(mesh):
    stream, cross = (mesh.shape["stream"], mesh.shape["cross"])
    sizes = (8, 4, 2, 12) if (stream, cross) == (16, 48) else (2, 2, stream // 2, cross // 2)
    return jax.shard_map(
        functools.partial(shards, sizes),
        mesh=mesh,
        in_specs=(
            P(None, None, "cross", "stream"),
            P(None, None, "cross", "stream"),
            P(None, None, "cross", None),
        ),
        out_specs=P(None, None, "cross", "stream"),
        check_vma=False,
    )
```

time: 74.8 us -> 39.5 us (0.53)
  the two profiles are of different devices: /device:TPU:1 before, /device:TPU:64 now
where the time goes in v1:
time: 39.5 us; the launch traced here: 39.3 us
  Pallas kernels  35 us (89%)
  local copies, waits for them, and re-layouts  3.21 us (8%)
  other arithmetic  1.05 us (3%)
    pallas_call x1, Pallas kernels, shards(): pl.pallas_call(functools.partial(kernel, sizes), out_shape=(jax.ShapeDtyp...  35 us
    transpose x1, local copies, waits for them, and re-layouts, shards(): now_t = jnp.transpose(state_now, (0, 2, 1, 3))  1.88 us
    add x1, other arithmetic, shards(): return state_base / 3.0 + 2.0 / 3.0 * (state_now + step * rate)  1.05 us

profile of v1, /device:TPU:64, one launch (start us, length us, event | category | flops | bytes accessed | tf_op | source)
XLA Modules:
  0.0 39.3 jit_solution(13854097182512883315)
XLA Ops:
  0.0 1.9 %copy_bitcast_fusion = (f32[7,8,8,128]{3,2,1,0:T(8,128)}, f32[7,8,8,128]{3,2,1,0:T(8,128)}) fusion(f32[7,8,8,128]{3,2,1,0:T(8,128)} %param.3, f32[7,8,8,128]{3,2,1,0:T(8,128)} %param.4), kind=kLoop, calls=%fused_computation.3 | loop fusion | bytes 917504 | tf_op jit(solution)/shard_map/transpose | solution.py:380
  1.9 0.0 copy-start
  1.9 0.0 copy-start.1
  1.9 35.0 %shard_map.37 = (f32[7,8,8,128]{3,2,1,0:T(8,128)}, f32[1,128]{1,0:T(1,128)}) custom-call(f32[7,8,8,128]{3,2,1,0:T(8,128)} %get-tuple-element.9.now_ref, f32[7,8,8,128]{3,2,1,0:T(8,128)} %get-tuple-element.10.base_ref, f32[7,3,8,8]{3,2,1,0:T(8,128)} %bitcast.13), custom_call_target="tpu_custom_call" | custom-call | tf_op jit(solution)/shard_map/pallas_call | solution.py:383
  36.9 0.0 copy-start.2
  36.9 0.6 %copy-done.2 = f32[1,128]{1,0:T(1,128)S(1)} copy-done((f32[1,128]{1,0:T(1,128)S(1)}, f32[1,128]{1,0:T(1,128)}, u32[]{:S(2)}) %copy-start.2) | copy-done | bytes 536
  37.5 0.0 copy-done
  37.5 0.0 copy-done.1
  37.6 1.1 %fusion.1 = f32[7,8,8,128]{3,1,2,0:T(8,128)S(1)} fusion(f32[7,8,8,128]{3,2,1,0:T(8,128)} %get-tuple-element.7, f32[7,8,8,128]{3,2,1,0:T(8,128)S(1)} %copy-done, f32[7,8,8,128]{3,2,1,0:T(8,128)S(1)} %copy-done.1, f32[]{:T(128)} %bitcast.3), kind=kLoop, calls=%fused_computation.2 | loop fusion | flops 286720 | bytes 917508 | tf_op jit(solution)/shard_map/add | solution.py:417
  38.6 0.7 %copy.8 = f32[7,8,8,128]{3,2,1,0:T(8,128)} copy(f32[7,8,8,128]{3,1,2,0:T(8,128)S(1)} %fusion.1) | data formatting | bytes 458752 | tf_op jit(solution)/shard_map/add | solution.py:417
Async XLA Ops:
  1.9 35.7 %copy-start = (f32[7,8,8,128]{3,2,1,0:T(8,128)S(1)}, f32[7,8,8,128]{3,2,1,0:T(8,128)}, u32[]{:S(2)}) copy-start(f32[7,8,8,128]{3,2,1,0:T(8,128)} %param.3) | copy-start | bytes 688132
  1.9 35.7 %copy-start.1 = (f32[7,8,8,128]{3,2,1,0:T(8,128)S(1)}, f32[7,8,8,128]{3,2,1,0:T(8,128)}, u32[]{:S(2)}) copy-start(f32[7,8,8,128]{3,2,1,0:T(8,128)} %param.4) | copy-start | bytes 688132
  36.9 0.6 %copy-start.2 = (f32[1,128]{1,0:T(1,128)S(1)}, f32[1,128]{1,0:T(1,128)}, u32[]{:S(2)}) copy-start(f32[1,128]{1,0:T(1,128)} %get-tuple-element.8) | copy-start | bytes 1540

commit v2 on v1

--- a/solution.py
+++ b/solution.py
@@ -147,6 +147,10 @@
     return outer_c, lambda k: (s, (c + k * inner_c) % (outer_c * inner_c))
 
 
+def far_first(n):
+    return sorted(range(1, n), key=lambda k: -min(k, n - k))
+
+
 def send(source, target, send_sem, recv_sem, to):
     return pltpu.make_async_remote_copy(
         src_ref=source,
@@ -165,8 +169,9 @@
     inflow_ref,
     rate_ref,
     fast_ref,
-    cells,
+    now,
     base,
+    halo,
     inflow,
     prim,
     xr,
@@ -193,23 +198,29 @@
     slots = (slots0, slots1, slots2)
     stages = [ring(k, sizes) for k in range(3)]
 
+    load_base = pltpu.make_async_copy(base_ref, base, in_sems.at[0])
+    load_now = pltpu.make_async_copy(now_ref, now, in_sems.at[1])
+    load_inflow = pltpu.make_async_copy(inflow_ref, inflow, in_sems.at[2])
+    load_base.start()
+    load_now.start()
+    load_inflow.start()
+
     barrier = pltpu.get_barrier_semaphore()
     count = 0
     for stage in (2, 1, 0):
         n, at = stages[stage]
-        for k in range(1, n):
+        for k in far_first(n):
             pl.semaphore_signal(barrier, inc=1, device_id=at(k), device_id_type=MESH)
             count += 1
     for there in (below, above, left, right):
         pl.semaphore_signal(barrier, inc=1, device_id=there, device_id_type=MESH)
         count += 1
 
-    load_base = pltpu.make_async_copy(base_ref, base, in_sems.at[0])
-    load_now = pltpu.make_async_copy(now_ref, cells.at[:, 3:11], in_sems.at[1])
-    load_inflow = pltpu.make_async_copy(inflow_ref, inflow, in_sems.at[2])
-    load_base.start()
-    load_now.start()
-    load_inflow.start()
+    now_rows = now.reshape(7, 64, 128)
+    halo_rows = halo.reshape(7, 64, 128)
+
+    def across_rows(ref, y):
+        return [ref[k, pl.ds(y, 8, stride=8), :] for k in range(7)]
 
     def all_of(ref, *index):
         return [ref[(k, *index)] for k in range(7)]
@@ -223,35 +234,11 @@
     load_base.wait()
     most = lax.fori_loop(0, 8, speed, jnp.zeros((8, 128), jnp.float32))
     rows[0] = jnp.broadcast_to(jnp.max(most, keepdims=True), (1, 128))
-    load_now.wait()
-    load_inflow.wait()
-
-    lane = lax.broadcasted_iota(jnp.int32, (8, 128), 1)
-    place = lane % 16
-    group = lane // 16
-    for k in range(7):
-        packed = rolled(cells[k, 3], 5, 1)
-        for y in range(1, 8):
-            packed = jnp.where(group == y, rolled(cells[k, 3 + y], 16 * y + 5, 1), packed)
-        a_own[k] = packed
-
-    def to_prim(y, _):
-        for k, value in enumerate(primitive(all_of(cells, y))):
-            prim[k, y] = value
-        return 0
-
     pl.semaphore_wait(barrier, count)
-
-    copies = [
-        send(cells.at[:, 3:6], cells.at[:, 11:14], halo_send.at[0], halo_recv.at[0], below),
-        send(cells.at[:, 8:11], cells.at[:, 0:3], halo_send.at[1], halo_recv.at[1], above),
-        send(a_own, a_right, halo_send.at[2], halo_recv.at[2], left),
-        send(a_own, a_left, halo_send.at[3], halo_recv.at[3], right),
-    ]
 
     def stage_start(stage):
         n, at = stages[stage]
-        for k in range(1, n):
+        for k in far_first(n):
             send(
                 rows.at[stage],
                 slots[stage].at[k - 1],
@@ -273,10 +260,43 @@
         return value
 
     stage_start(0)
+    load_now.wait()
+    load_inflow.wait()
+
+    lane = lax.broadcasted_iota(jnp.int32, (8, 128), 1)
+    place = lane % 16
+    group = lane // 16
+
+    def pack(y, packed):
+        packed = list(packed)
+        for k, value in enumerate(across_rows(now_rows, y)):
+            packed[k] = jnp.where(group == y, pltpu.roll(value, 16 * y + 5, 1), packed[k])
+        return tuple(packed)
+
+    packed = (jnp.zeros((8, 128), jnp.float32),) * 7
+    for y in range(8):
+        packed = pack(y, packed)
+    for k in range(7):
+        a_own[k] = packed[k]
+
+    copies = [
+        send(now.at[:, :, 0:3], halo.at[:, :, 0:3], halo_send.at[0], halo_recv.at[0], below),
+        send(now.at[:, :, 5:8], halo.at[:, :, 5:8], halo_send.at[1], halo_recv.at[1], above),
+        send(a_own, a_right, halo_send.at[2], halo_recv.at[2], left),
+        send(a_own, a_left, halo_send.at[3], halo_recv.at[3], right),
+    ]
     for copy in copies:
         copy.start()
 
-    lax.fori_loop(3, 11, to_prim, 0)
+    rows[1] = stage_end(0)
+    stage_start(1)
+
+    def own_prim(y, _):
+        for k, value in enumerate(primitive(across_rows(now_rows, y))):
+            prim[k, y + 3] = value
+        return 0
+
+    lax.fori_loop(0, 8, own_prim, 0)
 
     def local(y, _):
         w = all_of(prim, y + 3)
@@ -289,8 +309,8 @@
 
     lax.fori_loop(0, 8, local, 0)
 
-    rows[1] = stage_end(0)
-    stage_start(1)
+    rows[2] = stage_end(1)
+    stage_start(2)
 
     for copy in copies:
         copy.wait_recv()
@@ -323,8 +343,13 @@
     for k in range(7):
         edge[k] = jnp.where(place < 5, ends[k], rolled(ends[k], -6, 1))
 
-    lax.fori_loop(0, 3, to_prim, 0)
-    lax.fori_loop(11, 14, to_prim, 0)
+    def halo_prim(i, _):
+        row = i + i // 3 * 8
+        for k, value in enumerate(primitive(across_rows(halo_rows, (i + 5) % 8))):
+            prim[k, row] = value
+        return 0
+
+    lax.fori_loop(0, 6, halo_prim, 0)
 
     def cell_edges(y):
         upper, lower = ([], [])
@@ -335,7 +360,7 @@
             lower.append(two)
         return (upper, lower)
 
-    for k, value in enumerate(cell_edges(-1 + 0)[0]):
+    for k, value in enumerate(cell_edges(-1)[0]):
         xr[k] = value
     for k in range(8):
         flux_prev[k] = jnp.zeros((8, 128), jnp.float32)
@@ -358,14 +383,11 @@
 
     lax.fori_loop(0, 9, face, 0)
 
-    rows[2] = stage_end(1)
-    stage_start(2)
-
     near = (lane >= 125) | (lane <= 2)
     for k in range(7):
         for y in range(8):
             extra = jnp.where(near, rolled(edge[k], 123 - 16 * y, 1), 0.0)
-            rate_ref[k, y] = acc[k, y + 1] + extra
+            rate_ref[k, pl.ds(y, 8, stride=8), :] = acc[k, y + 1] + extra
 
     fast_ref[...] = stage_end(2)
     for copy in copies:
@@ -377,19 +399,18 @@
 def shards(sizes, state_now, state_base, inflow):
     size = jnp.float32
     n0, n1, n2 = (sizes[0], sizes[1] * sizes[2], sizes[3])
-    now_t = jnp.transpose(state_now, (0, 2, 1, 3))
-    base_t = jnp.transpose(state_base, (0, 2, 1, 3))
     inflow_t = jnp.transpose(inflow, (0, 3, 1, 2))
     rate, fast = pl.pallas_call(
         functools.partial(kernel, sizes),
         out_shape=(
-            jax.ShapeDtypeStruct((7, 8, 8, 128), size),
+            jax.ShapeDtypeStruct((7, 64, 128), size),
             jax.ShapeDtypeStruct((1, 128), size),
         ),
-        in_specs=[pl.BlockSpec(memory_space=pl.ANY)] * 3,
+        in_specs=[pl.BlockSpec(memory_space=pltpu.HBM)] * 3,
         out_specs=(pl.BlockSpec(memory_space=pltpu.VMEM),) * 2,
         scratch_shapes=[
-            pltpu.VMEM((7, 14, 8, 128), size),
+            pltpu.VMEM((7, 8, 8, 128), size),
+            pltpu.VMEM((7, 8, 8, 128), size),
             pltpu.VMEM((7, 8, 8, 128), size),
             pltpu.VMEM((7, 3, 8, 8), size),
             pltpu.VMEM((7, 14, 8, 128), size),
@@ -410,10 +431,16 @@
             pltpu.SemaphoreType.DMA((3,)),
             pltpu.SemaphoreType.DMA((3,)),
         ],
-        compiler_params=pltpu.CompilerParams(collective_id=0, has_side_effects=True),
-    )(now_t, base_t, inflow_t)
+        compiler_params=pltpu.CompilerParams(
+            collective_id=0, has_side_effects=True, vmem_limit_bytes=32 * 1024 * 1024
+        ),
+    )(
+        pltpu.with_memory_space_constraint(state_now, pltpu.HBM),
+        pltpu.with_memory_space_constraint(state_base, pltpu.HBM),
+        pltpu.with_memory_space_constraint(inflow_t, pltpu.HBM),
+    )
     step = 0.3 / fast[0, 0]
-    rate = jnp.transpose(rate, (0, 2, 1, 3)) * -0.5
+    rate = rate.reshape(state_now.shape) * -0.5
     return state_base / 3.0 + 2.0 / 3.0 * (state_now + step * rate)
 
 

time: 39.5 us -> 33.7 us (0.85)
  the two profiles are of different devices: /device:TPU:64 before, /device:TPU:1 now
where the time goes in v2:
time: 33.7 us; the launch traced here: 33.5 us
  Pallas kernels  32.7 us (97%)
  other arithmetic  0.75 us (2%)
    pallas_call x1, Pallas kernels, shards(): pl.pallas_call(functools.partial(kernel, sizes), out_shape=(jax.ShapeDtyp...  32.7 us
    add x1, other arithmetic, shards(): return state_base / 3.0 + 2.0 / 3.0 * (state_now + step * rate)  0.75 us

profile of v2, /device:TPU:1, one launch (start us, length us, event | category | flops | bytes accessed | tf_op | source)
XLA Modules:
  0.0 33.5 jit_solution(11587348369433954701)
XLA Ops:
  0.0 0.0 copy-start
  0.0 0.0 copy-start.1
  0.0 32.7 %shard_map.37 = (f32[7,64,128]{2,1,0:T(8,128)S(1)}, f32[1,128]{1,0:T(1,128)S(1)}) custom-call(f32[7,8,8,128]{3,2,1,0:T(8,128)} %now_ref.1, f32[7,8,8,128]{3,2,1,0:T(8,128)} %base_ref.1, f32[7,3,8,8]{3,2,1,0:T(8,128)} %bitcast.10), custom_call_target="tpu_custom_call" | custom-call | tf_op jit(solution)/shard_map/pallas_call | solution.py:403
  32.8 0.0 copy-done
  32.8 0.0 copy-done.1
  32.8 0.7 %fusion.1 = f32[7,8,8,128]{3,2,1,0:T(8,128)} fusion(f32[7,8,8,128]{3,2,1,0:T(8,128)S(1)} %copy-done, f32[7,64,128]{2,1,0:T(8,128)S(1)} %get-tuple-element.7, f32[7,8,8,128]{3,2,1,0:T(8,128)S(1)} %copy-done.1, f32[]{:T(128)} %bitcast.1), kind=kLoop, calls=%fused_computation.2 | loop fusion | flops 286720 | bytes 917508 | tf_op jit(solution)/shard_map/add | solution.py:444
Async XLA Ops:
  0.0 32.8 %copy-start = (f32[7,8,8,128]{3,2,1,0:T(8,128)S(1)}, f32[7,8,8,128]{3,2,1,0:T(8,128)}, u32[]{:S(2)}) copy-start(f32[7,8,8,128]{3,2,1,0:T(8,128)} %now_ref.1) | copy-start | bytes 688132
  0.0 32.8 %copy-start.1 = (f32[7,8,8,128]{3,2,1,0:T(8,128)S(1)}, f32[7,8,8,128]{3,2,1,0:T(8,128)}, u32[]{:S(2)}) copy-start(f32[7,8,8,128]{3,2,1,0:T(8,128)} %base_ref.1) | copy-start | bytes 688132

commit v3 on v2

--- a/solution.py
+++ b/solution.py
@@ -167,6 +167,7 @@
     now_ref,
     base_ref,
     inflow_ref,
+    part_ref,
     rate_ref,
     fast_ref,
     now,
@@ -185,6 +186,7 @@
     slots0,
     slots1,
     slots2,
+    told,
     in_sems,
     halo_send,
     halo_recv,
@@ -197,6 +199,10 @@
     below, above = ((s, (c + size_c - 1) % size_c), (s, (c + 1) % size_c))
     slots = (slots0, slots1, slots2)
     stages = [ring(k, sizes) for k in range(3)]
+    inner_c, planes = (sizes[1], sizes[3])
+    roots = max(1, planes // 3)
+    plane = c // inner_c
+    is_root = plane < roots
 
     load_base = pltpu.make_async_copy(base_ref, base, in_sems.at[0])
     load_now = pltpu.make_async_copy(now_ref, now, in_sems.at[1])
@@ -206,15 +212,19 @@
     load_inflow.start()
 
     barrier = pltpu.get_barrier_semaphore()
-    count = 0
-    for stage in (2, 1, 0):
-        n, at = stages[stage]
-        for k in far_first(n):
-            pl.semaphore_signal(barrier, inc=1, device_id=at(k), device_id_type=MESH)
-            count += 1
-    for there in (below, above, left, right):
+
+    def greet(there):
         pl.semaphore_signal(barrier, inc=1, device_id=there, device_id_type=MESH)
-        count += 1
+
+    for there in (left, right, below, above):
+        greet(there)
+
+    @pl.when(is_root)
+    def _():
+        for stage in (2, 1, 0):
+            n, at = stages[stage]
+            for k in far_first(n):
+                greet(at(k))
 
     now_rows = now.reshape(7, 64, 128)
     halo_rows = halo.reshape(7, 64, 128)
@@ -233,8 +243,14 @@
 
     load_base.wait()
     most = lax.fori_loop(0, 8, speed, jnp.zeros((8, 128), jnp.float32))
-    rows[0] = jnp.broadcast_to(jnp.max(most, keepdims=True), (1, 128))
-    pl.semaphore_wait(barrier, count)
+    rows[2] = jnp.broadcast_to(jnp.max(most, keepdims=True), (1, 128))
+    @pl.when(is_root)
+    def _():
+        pl.semaphore_wait(barrier, 4 + roots - 1 + stages[1][0] - 1 + stages[0][0] - 1)
+
+    @pl.when(jnp.logical_not(is_root))
+    def _():
+        pl.semaphore_wait(barrier, 4 + roots)
 
     def stage_start(stage):
         n, at = stages[stage]
@@ -259,7 +275,21 @@
             value = jnp.maximum(value, slots[stage][k - 1])
         return value
 
-    stage_start(0)
+    def to_root(root):
+        return send(
+            rows.at[2],
+            slots2.at[(root - plane + planes) % planes - 1],
+            stage_send.at[2],
+            stage_recv.at[2],
+            (s, root * inner_c + c % inner_c),
+        )
+
+    for root in range(roots):
+
+        @pl.when(plane != root)
+        def _(root=root):
+            to_root(root).start()
+
     load_now.wait()
     load_inflow.wait()
 
@@ -288,9 +318,6 @@
     for copy in copies:
         copy.start()
 
-    rows[1] = stage_end(0)
-    stage_start(1)
-
     def own_prim(y, _):
         for k, value in enumerate(primitive(across_rows(now_rows, y))):
             prim[k, y + 3] = value
@@ -309,8 +336,19 @@
 
     lax.fori_loop(0, 8, local, 0)
 
-    rows[2] = stage_end(1)
-    stage_start(2)
+    def fixed_part(z, _):
+        for k in range(7):
+            part_ref[k, z] = base[k, z] * (1.0 / 3.0) + now[k, z] * (2.0 / 3.0)
+        return 0
+
+    lax.fori_loop(0, 8, fixed_part, 0)
+
+    @pl.when(is_root)
+    def _():
+        rows[1] = stage_end(2)
+        stage_start(1)
+        rows[0] = stage_end(1)
+        stage_start(0)
 
     for copy in copies:
         copy.wait_recv()
@@ -387,27 +425,64 @@
     for k in range(7):
         for y in range(8):
             extra = jnp.where(near, rolled(edge[k], 123 - 16 * y, 1), 0.0)
-            rate_ref[k, pl.ds(y, 8, stride=8), :] = acc[k, y + 1] + extra
-
-    fast_ref[...] = stage_end(2)
+            rate_ref[k, pl.ds(y, 8, stride=8), :] = (acc[k, y + 1] + extra) * (-1.0 / 3.0)
+
+    children = [
+        send(
+            rows.at[3],
+            told.at[0],
+            stage_send.at[3],
+            stage_recv.at[3],
+            (s, (c + k * roots * inner_c) % size_c),
+        )
+        for k in range(1, planes // roots)
+    ]
+
+    @pl.when(is_root)
+    def _():
+        rows[3] = stage_end(0)
+        for copy in children:
+            copy.start()
+        fast_ref[...] = rows[3]
+
+    @pl.when(jnp.logical_not(is_root))
+    def _():
+        children[0].wait_recv()
+        fast_ref[...] = told[0]
+
     for copy in copies:
         copy.wait_send()
-    for stage in range(3):
-        stage_total(stage).wait_send()
+
+    def sent(count, stage):
+        span = slots2.at[pl.ds(0, count)]
+        send(span, span, stage_send.at[stage], stage_recv.at[stage], right).wait_send()
+
+    @pl.when(is_root)
+    def _():
+        for stage in range(2):
+            stage_total(stage).wait_send()
+        if roots > 1:
+            sent(roots - 1, 2)
+        sent(planes // roots - 1, 3)
+
+    @pl.when(jnp.logical_not(is_root))
+    def _():
+        sent(roots, 2)
 
 
 def shards(sizes, state_now, state_base, inflow):
     size = jnp.float32
     n0, n1, n2 = (sizes[0], sizes[1] * sizes[2], sizes[3])
     inflow_t = jnp.transpose(inflow, (0, 3, 1, 2))
-    rate, fast = pl.pallas_call(
+    part, rate, fast = pl.pallas_call(
         functools.partial(kernel, sizes),
         out_shape=(
+            jax.ShapeDtypeStruct((7, 8, 8, 128), size),
             jax.ShapeDtypeStruct((7, 64, 128), size),
             jax.ShapeDtypeStruct((1, 128), size),
         ),
         in_specs=[pl.BlockSpec(memory_space=pltpu.HBM)] * 3,
-        out_specs=(pl.BlockSpec(memory_space=pltpu.VMEM),) * 2,
+        out_specs=(pl.BlockSpec(memory_space=pltpu.VMEM),) * 3,
         scratch_shapes=[
             pltpu.VMEM((7, 8, 8, 128), size),
             pltpu.VMEM((7, 8, 8, 128), size),
@@ -421,15 +496,16 @@
             pltpu.VMEM((7, 8, 128), size),
             pltpu.VMEM((7, 8, 128), size),
             pltpu.VMEM((7, 8, 128), size),
-            pltpu.VMEM((3, 1, 128), size),
+            pltpu.VMEM((4, 1, 128), size),
             pltpu.VMEM((n0 - 1, 1, 128), size),
             pltpu.VMEM((n1 - 1, 1, 128), size),
             pltpu.VMEM((n2 - 1, 1, 128), size),
+            pltpu.VMEM((1, 1, 128), size),
             pltpu.SemaphoreType.DMA((3,)),
             pltpu.SemaphoreType.DMA((4,)),
             pltpu.SemaphoreType.DMA((4,)),
-            pltpu.SemaphoreType.DMA((3,)),
-            pltpu.SemaphoreType.DMA((3,)),
+            pltpu.SemaphoreType.DMA((4,)),
+            pltpu.SemaphoreType.DMA((4,)),
         ],
         compiler_params=pltpu.CompilerParams(
             collective_id=0, has_side_effects=True, vmem_limit_bytes=32 * 1024 * 1024
@@ -439,9 +515,7 @@
         pltpu.with_memory_space_constraint(state_base, pltpu.HBM),
         pltpu.with_memory_space_constraint(inflow_t, pltpu.HBM),
     )
-    step = 0.3 / fast[0, 0]
-    rate = rate.reshape(state_now.shape) * -0.5
-    return state_base / 3.0 + 2.0 / 3.0 * (state_now + step * rate)
+    return part + 0.3 / fast[0, 0] * rate.reshape(state_now.shape)
 
 
 def solution(mesh):

time: 33.7 us -> 32.3 us (0.958)
  Pallas kernels: 32.7 us -> 31.3 us
    pallas_call x1, Pallas kernels: 32.7 us -> 31.3 us  [shards(): pl.pallas_call(functools.partial(kernel, sizes), out_shape=(jax.ShapeDtyp...]
where the time goes in v3:
time: 32.3 us; the launch traced here: 32.1 us
  Pallas kernels  31.3 us (97%)
  other arithmetic  0.72 us (2%)
    pallas_call x1, Pallas kernels, shards(): pl.pallas_call(functools.partial(kernel, sizes), out_shape=(jax.ShapeDtyp...  31.3 us
    add x1, other arithmetic, shards(): return part + 0.3 / fast[0, 0] * rate.reshape(state_now.shape)  0.72 us

profile of v3, /device:TPU:1, one launch (start us, length us, event | category | flops | bytes accessed | tf_op | source)
XLA Modules:
  0.0 32.1 jit_solution(18241308087168244928)
XLA Ops:
  0.0 31.3 %shard_map.37 = (f32[7,8,8,128]{3,2,1,0:T(8,128)S(1)}, f32[7,64,128]{2,1,0:T(8,128)S(1)}, f32[1,128]{1,0:T(1,128)S(1)}) custom-call(f32[7,8,8,128]{3,2,1,0:T(8,128)} %now_ref.1, f32[7,8,8,128]{3,2,1,0:T(8,128)} %base_ref.1, f32[7,3,8,8]{3,2,1,0:T(8,128)} %bitcast.6), custom_call_target="tpu_custom_call" | custom-call | tf_op jit(solution)/shard_map/pallas_call | solution.py:477
  31.4 0.7 %bitcast_add_fusion = f32[7,8,8,128]{3,2,1,0:T(8,128)} fusion(f32[7,8,8,128]{3,2,1,0:T(8,128)S(1)} %get-tuple-element.8, f32[7,64,128]{2,1,0:T(8,128)S(1)} %get-tuple-element.10, f32[]{:T(128)} %bitcast.1), kind=kLoop, calls=%fused_computation | loop fusion | flops 114688 | bytes 688132 | tf_op jit(solution)/shard_map/add | solution.py:518

commit v4 on v3

--- a/solution.py
+++ b/solution.py
@@ -216,8 +216,22 @@
     def greet(there):
         pl.semaphore_signal(barrier, inc=1, device_id=there, device_id_type=MESH)
 
-    for there in (left, right, below, above):
-        greet(there)
+    first_s, last_s = (s % sizes[0] == 0, s % sizes[0] == sizes[0] - 1)
+    first_c, last_c = (c % inner_c == 0, c % inner_c == inner_c - 1)
+    flip = s // sizes[0] > 0
+    answer_left = first_s
+    answer_above = last_c & flip
+    answer_below = first_c & jnp.logical_not(flip)
+    greet(left)
+    pl.when(jnp.logical_not(last_s))(lambda: greet(right))
+    pl.when(jnp.logical_not(first_c & flip))(lambda: greet(below))
+    pl.when(jnp.logical_not(last_c & jnp.logical_not(flip)))(lambda: greet(above))
+    greeted = (
+        1
+        + jnp.where(answer_left, 0, 1)
+        + jnp.where(answer_above, 0, 1)
+        + jnp.where(answer_below, 0, 1)
+    )
 
     @pl.when(is_root)
     def _():
@@ -242,16 +256,10 @@
         return jnp.maximum(most, swift + sound(w[0] + w[1], w[5], gamma, stiff))
 
     load_base.wait()
-    most = lax.fori_loop(0, 8, speed, jnp.zeros((8, 128), jnp.float32))
+    most = jnp.zeros((8, 128), jnp.float32)
+    for y in range(8):
+        most = speed(y, most)
     rows[2] = jnp.broadcast_to(jnp.max(most, keepdims=True), (1, 128))
-    @pl.when(is_root)
-    def _():
-        pl.semaphore_wait(barrier, 4 + roots - 1 + stages[1][0] - 1 + stages[0][0] - 1)
-
-    @pl.when(jnp.logical_not(is_root))
-    def _():
-        pl.semaphore_wait(barrier, 4 + roots)
-
     def stage_start(stage):
         n, at = stages[stage]
         for k in far_first(n):
@@ -284,12 +292,6 @@
             (s, root * inner_c + c % inner_c),
         )
 
-    for root in range(roots):
-
-        @pl.when(plane != root)
-        def _(root=root):
-            to_root(root).start()
-
     load_now.wait()
     load_inflow.wait()
 
@@ -315,15 +317,10 @@
         send(a_own, a_right, halo_send.at[2], halo_recv.at[2], left),
         send(a_own, a_left, halo_send.at[3], halo_recv.at[3], right),
     ]
-    for copy in copies:
-        copy.start()
-
     def own_prim(y, _):
         for k, value in enumerate(primitive(across_rows(now_rows, y))):
             prim[k, y + 3] = value
         return 0
-
-    lax.fori_loop(0, 8, own_prim, 0)
 
     def local(y, _):
         w = all_of(prim, y + 3)
@@ -334,52 +331,66 @@
             acc[k, y + 1] = across[k] + stream[k]
         return 0
 
-    lax.fori_loop(0, 8, local, 0)
-
     def fixed_part(z, _):
         for k in range(7):
             part_ref[k, z] = base[k, z] * (1.0 / 3.0) + now[k, z] * (2.0 / 3.0)
         return 0
 
-    lax.fori_loop(0, 8, fixed_part, 0)
+    def at_home():
+        lax.fori_loop(0, 8, own_prim, 0)
+        lax.fori_loop(0, 8, local, 0)
+        lax.fori_loop(0, 8, fixed_part, 0)
+
+    pl.when(is_root)(at_home)
+
+    @pl.when(is_root)
+    def _():
+        pl.semaphore_wait(barrier, greeted + roots - 1 + stages[1][0] - 1 + stages[0][0] - 1)
+
+    @pl.when(jnp.logical_not(is_root))
+    def _():
+        pl.semaphore_wait(barrier, greeted + roots)
+
+    for root in range(roots):
+
+        @pl.when(plane != root)
+        def _(root=root):
+            to_root(root).start()
+
+    copies[3].start()
+    pl.when(jnp.logical_not(answer_left))(copies[2].start)
+    pl.when(jnp.logical_not(answer_above))(copies[1].start)
+    pl.when(jnp.logical_not(answer_below))(copies[0].start)
+
+    pl.when(jnp.logical_not(is_root))(at_home)
+
+    @pl.when(answer_below)
+    def _():
+        copies[1].wait_recv()
+        copies[0].start()
+
+    @pl.when(answer_above)
+    def _():
+        copies[0].wait_recv()
+        copies[1].start()
+
+    @pl.when(answer_left)
+    def _():
+        copies[3].wait_recv()
+        copies[2].start()
 
     @pl.when(is_root)
     def _():
         rows[1] = stage_end(2)
         stage_start(1)
+
+    @pl.when(is_root)
+    def _():
         rows[0] = stage_end(1)
         stage_start(0)
 
-    for copy in copies:
-        copy.wait_recv()
-
-    @pl.when(s == 0)
-    def _():
-        for k in range(7):
-            value = jnp.zeros((8, 128), jnp.float32)
-            for layer in range(3):
-                for y in range(8):
-                    one = jnp.broadcast_to(inflow[k, layer][:, y : y + 1], (8, 128))
-                    value = jnp.where((group == y) & (place == 2 + layer), one, value)
-            a_left[k] = value
-
-    @pl.when(s == size_s - 1)
-    def _():
-        for k in range(7):
-            value = a_own[k]
-            one, two, three = (rolled(value, 1, 1), rolled(value, 2, 1), rolled(value, 3, 1))
-            a_right[k] = jnp.where(place == 5, one, jnp.where(place == 6, two, three))
-
-    rim = []
-    for k in range(7):
-        own = a_own[k]
-        late = rolled(jnp.where(place < 5, a_left[k], own), 6, 1)
-        rim.append(jnp.where(place < 5, own, jnp.where(place < 8, a_right[k], late)))
-    w = primitive(rim)
-    keep = ((place >= 3) & (place <= 5)) | ((place >= 11) & (place <= 13))
-    ends = folded(spread(along(w, 1, 0), 1, keep), w[6])
-    for k in range(7):
-        edge[k] = jnp.where(place < 5, ends[k], rolled(ends[k], -6, 1))
+    pl.when(jnp.logical_not(answer_below))(copies[1].wait_recv)
+    pl.when(jnp.logical_not(answer_above))(copies[0].wait_recv)
 
     def halo_prim(i, _):
         row = i + i // 3 * 8
@@ -421,6 +432,37 @@
 
     lax.fori_loop(0, 9, face, 0)
 
+    copies[2].wait_recv()
+    pl.when(jnp.logical_not(answer_left))(copies[3].wait_recv)
+
+    @pl.when(s == 0)
+    def _():
+        for k in range(7):
+            value = jnp.zeros((8, 128), jnp.float32)
+            for layer in range(3):
+                for y in range(8):
+                    one = jnp.broadcast_to(inflow[k, layer][:, y : y + 1], (8, 128))
+                    value = jnp.where((group == y) & (place == 2 + layer), one, value)
+            a_left[k] = value
+
+    @pl.when(s == size_s - 1)
+    def _():
+        for k in range(7):
+            value = a_own[k]
+            one, two, three = (rolled(value, 1, 1), rolled(value, 2, 1), rolled(value, 3, 1))
+            a_right[k] = jnp.where(place == 5, one, jnp.where(place == 6, two, three))
+
+    rim = []
+    for k in range(7):
+        own = a_own[k]
+        late = rolled(jnp.where(place < 5, a_left[k], own), 6, 1)
+        rim.append(jnp.where(place < 5, own, jnp.where(place < 8, a_right[k], late)))
+    w = primitive(rim)
+    keep = ((place >= 3) & (place <= 5)) | ((place >= 11) & (place <= 13))
+    ends = folded(spread(along(w, 1, 0), 1, keep), w[6])
+    for k in range(7):
+        edge[k] = jnp.where(place < 5, ends[k], rolled(ends[k], -6, 1))
+
     near = (lane >= 125) | (lane <= 2)
     for k in range(7):
         for y in range(8):
@@ -433,17 +475,21 @@
             told.at[0],
             stage_send.at[3],
             stage_recv.at[3],
-            (s, (c + k * roots * inner_c) % size_c),
+            (s, (c + k * inner_c) % size_c),
         )
-        for k in range(1, planes // roots)
+        for k in range(1, planes - roots + 1)
     ]
 
     @pl.when(is_root)
     def _():
-        rows[3] = stage_end(0)
+        fastest = stage_end(0)
+        rows[3] = fastest
+        fast_ref[...] = fastest
+
+    @pl.when(plane == roots - 1)
+    def _():
         for copy in children:
             copy.start()
-        fast_ref[...] = rows[3]
 
     @pl.when(jnp.logical_not(is_root))
     def _():
@@ -463,7 +509,10 @@
             stage_total(stage).wait_send()
         if roots > 1:
             sent(roots - 1, 2)
-        sent(planes // roots - 1, 3)
+
+    @pl.when(plane == roots - 1)
+    def _():
+        sent(planes - roots, 3)
 
     @pl.when(jnp.logical_not(is_root))
     def _():

time: 32.3 us -> 31.2 us (0.966)
  Pallas kernels: 31.3 us -> 30.3 us
    pallas_call x1, Pallas kernels: 31.3 us -> 30.3 us  [shards(): pl.pallas_call(functools.partial(kernel, sizes), out_shape=(jax.ShapeDtyp...]
where the time goes in v4:
time: 31.2 us; the launch traced here: 31.1 us
  Pallas kernels  30.3 us (97%)
  other arithmetic  0.72 us (2%)
    pallas_call x1, Pallas kernels, shards(): pl.pallas_call(functools.partial(kernel, sizes), out_shape=(jax.ShapeDtyp...  30.3 us
    add x1, other arithmetic, shards(): return part + 0.3 / fast[0, 0] * rate.reshape(state_now.shape)  0.72 us

profile of v4, /device:TPU:1, one launch (start us, length us, event | category | flops | bytes accessed | tf_op | source)
XLA Modules:
  0.0 31.1 jit_solution(10376196944082594743)
XLA Ops:
  0.0 30.3 %shard_map.37 = (f32[7,8,8,128]{3,2,1,0:T(8,128)S(1)}, f32[7,64,128]{2,1,0:T(8,128)S(1)}, f32[1,128]{1,0:T(1,128)S(1)}) custom-call(f32[7,8,8,128]{3,2,1,0:T(8,128)} %now_ref.1, f32[7,8,8,128]{3,2,1,0:T(8,128)} %base_ref.1, f32[7,3,8,8]{3,2,1,0:T(8,128)} %bitcast.6), custom_call_target="tpu_custom_call" | custom-call | tf_op jit(solution)/shard_map/pallas_call | solution.py:526
  30.4 0.7 %bitcast_add_fusion = f32[7,8,8,128]{3,2,1,0:T(8,128)} fusion(f32[7,8,8,128]{3,2,1,0:T(8,128)S(1)} %get-tuple-element.8, f32[7,64,128]{2,1,0:T(8,128)S(1)} %get-tuple-element.10, f32[]{:T(128)} %bitcast.1), kind=kLoop, calls=%fused_computation | loop fusion | flops 114688 | bytes 688132 | tf_op jit(solution)/shard_map/add | solution.py:567

commit v5 on v4

--- a/solution.py
+++ b/solution.py
@@ -169,7 +169,7 @@
     inflow_ref,
     part_ref,
     rate_ref,
-    fast_ref,
+    step_ref,
     now,
     base,
     halo,
@@ -187,6 +187,7 @@
     slots1,
     slots2,
     told,
+    quick,
     in_sems,
     halo_send,
     halo_recv,
@@ -222,12 +223,29 @@
     answer_left = first_s
     answer_above = last_c & flip
     answer_below = first_c & jnp.logical_not(flip)
+    chief_s, chief_c = (1, 0)
+    in_first = plane == 0
+    is_chief = (s == chief_s) & (c == chief_c)
+    serves_chief = in_first & jnp.logical_not(is_chief)
+    beside_chief = serves_chief & (s // sizes[0] == chief_s // sizes[0]) & (c == chief_c)
+    members = size_s * inner_c
+
     greet(left)
     pl.when(jnp.logical_not(last_s))(lambda: greet(right))
     pl.when(jnp.logical_not(first_c & flip))(lambda: greet(below))
     pl.when(jnp.logical_not(last_c & jnp.logical_not(flip)))(lambda: greet(above))
+
+    @pl.when(is_chief)
+    def _():
+        def greet_member(k, _):
+            pl.when(k != chief_s * inner_c + chief_c)(lambda: greet((k // inner_c, k % inner_c)))
+            return 0
+
+        lax.fori_loop(0, members, greet_member, 0)
+
     greeted = (
         1
+        + jnp.where(serves_chief, 1, 0)
         + jnp.where(answer_left, 0, 1)
         + jnp.where(answer_above, 0, 1)
         + jnp.where(answer_below, 0, 1)
@@ -263,13 +281,18 @@
     def stage_start(stage):
         n, at = stages[stage]
         for k in far_first(n):
-            send(
+            copy = send(
                 rows.at[stage],
                 slots[stage].at[k - 1],
                 stage_send.at[stage],
                 stage_recv.at[stage],
                 at(k),
-            ).start()
+            )
+            if stage == 0:
+                there_s, there_c = at(k)
+                pl.when((there_s != chief_s) | (there_c != chief_c))(copy.start)
+            else:
+                copy.start()
 
     def stage_total(stage):
         n, at = stages[stage]
@@ -291,6 +314,12 @@
             stage_recv.at[2],
             (s, root * inner_c + c % inner_c),
         )
+
+    @pl.when(jnp.logical_not(is_root))
+    def _():
+        pl.semaphore_wait(barrier, greeted + roots)
+        for root in range(roots):
+            to_root(root).start()
 
     load_now.wait()
     load_inflow.wait()
@@ -346,23 +375,28 @@
     @pl.when(is_root)
     def _():
         pl.semaphore_wait(barrier, greeted + roots - 1 + stages[1][0] - 1 + stages[0][0] - 1)
-
-    @pl.when(jnp.logical_not(is_root))
-    def _():
-        pl.semaphore_wait(barrier, greeted + roots)
-
-    for root in range(roots):
-
-        @pl.when(plane != root)
-        def _(root=root):
-            to_root(root).start()
+        for root in range(roots):
+            pl.when(plane != root)(to_root(root).start)
 
     copies[3].start()
     pl.when(jnp.logical_not(answer_left))(copies[2].start)
     pl.when(jnp.logical_not(answer_above))(copies[1].start)
     pl.when(jnp.logical_not(answer_below))(copies[0].start)
 
+    to_chief = send(
+        rows.at[1],
+        quick.at[s * inner_c + c % inner_c],
+        stage_send.at[4],
+        stage_recv.at[4],
+        (chief_s, chief_c),
+    )
     pl.when(jnp.logical_not(is_root))(at_home)
+
+    @pl.when(is_root)
+    def _():
+        rows[1] = stage_end(2)
+        pl.when(serves_chief)(to_chief.start)
+        stage_start(1)
 
     @pl.when(answer_below)
     def _():
@@ -378,11 +412,6 @@
     def _():
         copies[3].wait_recv()
         copies[2].start()
-
-    @pl.when(is_root)
-    def _():
-        rows[1] = stage_end(2)
-        stage_start(1)
 
     @pl.when(is_root)
     def _():
@@ -480,11 +509,22 @@
         for k in range(1, planes - roots + 1)
     ]
 
-    @pl.when(is_root)
+    @pl.when(is_root & jnp.logical_not(is_chief))
     def _():
         fastest = stage_end(0)
         rows[3] = fastest
-        fast_ref[...] = fastest
+        step_ref[...] = 0.3 / fastest
+
+    @pl.when(is_chief)
+    def _():
+        span = quick.at[pl.ds(0, members - 1)]
+        send(span, span, stage_send.at[4], stage_recv.at[4], right).wait_recv()
+        fastest = rows[1]
+        for k in range(members):
+            if k != chief_s * inner_c + chief_c:
+                fastest = jnp.maximum(fastest, quick[k])
+        rows[3] = fastest
+        step_ref[...] = 0.3 / fastest
 
     @pl.when(plane == roots - 1)
     def _():
@@ -494,7 +534,7 @@
     @pl.when(jnp.logical_not(is_root))
     def _():
         children[0].wait_recv()
-        fast_ref[...] = told[0]
+        step_ref[...] = 0.3 / told[0]
 
     for copy in copies:
         copy.wait_send()
@@ -505,11 +545,20 @@
 
     @pl.when(is_root)
     def _():
-        for stage in range(2):
-            stage_total(stage).wait_send()
+        stage_total(1).wait_send()
         if roots > 1:
             sent(roots - 1, 2)
 
+    pl.when(is_root & jnp.logical_not(beside_chief))(stage_total(0).wait_send)
+
+    @pl.when(beside_chief)
+    def _():
+        if sizes[0] > 2:
+            span = slots0.at[pl.ds(0, sizes[0] - 2)]
+            send(span, span, stage_send.at[0], stage_recv.at[0], right).wait_send()
+
+    pl.when(serves_chief)(to_chief.wait_send)
+
     @pl.when(plane == roots - 1)
     def _():
         sent(planes - roots, 3)
@@ -521,9 +570,10 @@
 
 def shards(sizes, state_now, state_base, inflow):
     size = jnp.float32
+    stream = sizes[0] * sizes[2]
     n0, n1, n2 = (sizes[0], sizes[1] * sizes[2], sizes[3])
     inflow_t = jnp.transpose(inflow, (0, 3, 1, 2))
-    part, rate, fast = pl.pallas_call(
+    part, rate, step = pl.pallas_call(
         functools.partial(kernel, sizes),
         out_shape=(
             jax.ShapeDtypeStruct((7, 8, 8, 128), size),
@@ -550,11 +600,12 @@
             pltpu.VMEM((n1 - 1, 1, 128), size),
             pltpu.VMEM((n2 - 1, 1, 128), size),
             pltpu.VMEM((1, 1, 128), size),
+            pltpu.VMEM((n1 // sizes[2] * stream, 1, 128), size),
             pltpu.SemaphoreType.DMA((3,)),
             pltpu.SemaphoreType.DMA((4,)),
             pltpu.SemaphoreType.DMA((4,)),
-            pltpu.SemaphoreType.DMA((4,)),
-            pltpu.SemaphoreType.DMA((4,)),
+            pltpu.SemaphoreType.DMA((5,)),
+            pltpu.SemaphoreType.DMA((5,)),
         ],
         compiler_params=pltpu.CompilerParams(
             collective_id=0, has_side_effects=True, vmem_limit_bytes=32 * 1024 * 1024
@@ -564,7 +615,7 @@
         pltpu.with_memory_space_constraint(state_base, pltpu.HBM),
         pltpu.with_memory_space_constraint(inflow_t, pltpu.HBM),
     )
-    return part + 0.3 / fast[0, 0] * rate.reshape(state_now.shape)
+    return part + step.reshape(1, 1, 1, 128) * rate.reshape(state_now.shape)
 
 
 def solution(mesh):

time: 31.2 us -> 29.6 us (0.949)
  the two profiles are of different devices: /device:TPU:1 before, /device:TPU:8 now
where the time goes in v5:
time: 29.6 us; the launch traced here: 29.5 us
  Pallas kernels  28.8 us (97%)
  other arithmetic  0.72 us (2%)
    pallas_call x1, Pallas kernels, shards(): pl.pallas_call(functools.partial(kernel, sizes), out_shape=(jax.ShapeDtyp...  28.8 us
    add x1, other arithmetic, shards(): return part + step.reshape(1, 1, 1, 128) * rate.reshape(state_now.shape)  0.72 us

profile of v5, /device:TPU:8, one launch (start us, length us, event | category | flops | bytes accessed | tf_op | source)
XLA Modules:
  0.0 29.5 jit_solution(15534405803175192679)
XLA Ops:
  0.0 28.8 %shard_map.37 = (f32[7,8,8,128]{3,2,1,0:T(8,128)S(1)}, f32[7,64,128]{2,1,0:T(8,128)S(1)}, f32[1,128]{1,0:T(1,128)S(1)}) custom-call(f32[7,8,8,128]{3,2,1,0:T(8,128)} %now_ref.1, f32[7,8,8,128]{3,2,1,0:T(8,128)} %base_ref.1, f32[7,3,8,8]{3,2,1,0:T(8,128)} %bitcast.7), custom_call_target="tpu_custom_call" | custom-call | tf_op jit(solution)/shard_map/pallas_call | solution.py:576
  28.8 0.7 %fusion = f32[7,8,8,128]{3,2,1,0:T(8,128)} fusion(f32[7,8,8,128]{3,2,1,0:T(8,128)S(1)} %get-tuple-element.8, f32[7,64,128]{2,1,0:T(8,128)S(1)} %get-tuple-element.10, f32[128]{0:T(128)S(1)} %bitcast.6), kind=kLoop, calls=%fused_computation.1 | loop fusion | flops 114688 | bytes 688640 | tf_op jit(solution)/shard_map/add | solution.py:618

commit v6 on v4

--- a/solution.py
+++ b/solution.py
@@ -126,29 +126,34 @@
     return change[:6] + [change[6] - volume * change[7]]
 
 
-def ring(stage, sizes):
-    inner_s, inner_c, outer_s, outer_c = sizes
+def in_plane(sizes):
+    inner_s, inner_c, outer_s, _ = sizes
     s, c = (lax.axis_index("stream"), lax.axis_index("cross"))
-    if stage == 0:
-        base = s // inner_s * inner_s
-        return inner_s, lambda k: (base + (s - base + k) % inner_s, c)
-    if stage == 1:
-        n = outer_s * inner_c
-        place = s // inner_s * inner_c + c % inner_c
-
-        def at(k):
-            there = (place + k) % n
-            return (
-                there // inner_c * inner_s + s % inner_s,
-                c // inner_c * inner_c + there % inner_c,
+    length = outer_s * inner_c
+    x, y = (s % inner_s, s // inner_s * inner_c + c % inner_c)
+    offsets = [(i, j) for i in range(inner_s) for j in range(length) if i or j]
+
+    def distance(offset):
+        i, j = offset
+        return min(i, inner_s - i) / 2 + min(j, length - j)
+
+    there = []
+    for i, j in sorted(offsets, key=lambda offset: -distance(offset)):
+        y_there = (y + j) % length
+        there.append(
+            (
+                y_there // inner_c * inner_s + (x + i) % inner_s,
+                c // inner_c * inner_c + y_there % inner_c,
             )
-
-        return n, at
-    return outer_c, lambda k: (s, (c + k * inner_c) % (outer_c * inner_c))
-
-
-def far_first(n):
-    return sorted(range(1, n), key=lambda k: -min(k, n - k))
+        )
+    return there
+
+
+def along_z(sizes):
+    _, inner_c, _, planes = sizes
+    s, c = (lax.axis_index("stream"), lax.axis_index("cross"))
+    offsets = sorted(range(1, planes), key=lambda k: -min(k, planes - k))
+    return [(s, (c + k * inner_c) % (planes * inner_c)) for k in offsets]
 
 
 def send(source, target, send_sem, recv_sem, to):
@@ -169,7 +174,7 @@
     inflow_ref,
     part_ref,
     rate_ref,
-    fast_ref,
+    step_ref,
     now,
     base,
     halo,
@@ -183,9 +188,8 @@
     a_right,
     edge,
     rows,
-    slots0,
-    slots1,
-    slots2,
+    slots_z,
+    slots_p,
     told,
     in_sems,
     halo_send,
@@ -197,8 +201,7 @@
     s, c = (lax.axis_index("stream"), lax.axis_index("cross"))
     left, right = (((s + size_s - 1) % size_s, c), ((s + 1) % size_s, c))
     below, above = ((s, (c + size_c - 1) % size_c), (s, (c + 1) % size_c))
-    slots = (slots0, slots1, slots2)
-    stages = [ring(k, sizes) for k in range(3)]
+    mates, others = (in_plane(sizes), along_z(sizes))
     inner_c, planes = (sizes[1], sizes[3])
     roots = max(1, planes // 3)
     plane = c // inner_c
@@ -235,10 +238,8 @@
 
     @pl.when(is_root)
     def _():
-        for stage in (2, 1, 0):
-            n, at = stages[stage]
-            for k in far_first(n):
-                greet(at(k))
+        for there in others + mates:
+            greet(there)
 
     now_rows = now.reshape(7, 64, 128)
     halo_rows = halo.reshape(7, 64, 128)
@@ -259,38 +260,27 @@
     most = jnp.zeros((8, 128), jnp.float32)
     for y in range(8):
         most = speed(y, most)
-    rows[2] = jnp.broadcast_to(jnp.max(most, keepdims=True), (1, 128))
-    def stage_start(stage):
-        n, at = stages[stage]
-        for k in far_first(n):
-            send(
-                rows.at[stage],
-                slots[stage].at[k - 1],
-                stage_send.at[stage],
-                stage_recv.at[stage],
-                at(k),
-            ).start()
-
-    def stage_total(stage):
-        n, at = stages[stage]
-        return send(slots[stage], slots[stage], stage_send.at[stage], stage_recv.at[stage], at(1))
-
-    def stage_end(stage):
-        n, _ = stages[stage]
-        stage_total(stage).wait_recv()
-        value = rows[stage]
-        for k in range(1, n):
-            value = jnp.maximum(value, slots[stage][k - 1])
-        return value
+    rows[0] = jnp.broadcast_to(jnp.max(most, keepdims=True), (1, 128))
+    def arrived(slots, stage, own):
+        send(slots, slots, stage_send.at[stage], stage_recv.at[stage], right).wait_recv()
+        for k in range(slots.shape[0]):
+            own = jnp.maximum(own, slots[k])
+        return own
 
     def to_root(root):
         return send(
-            rows.at[2],
-            slots2.at[(root - plane + planes) % planes - 1],
-            stage_send.at[2],
-            stage_recv.at[2],
+            rows.at[0],
+            slots_z.at[(root - plane + planes) % planes - 1],
+            stage_send.at[0],
+            stage_recv.at[0],
             (s, root * inner_c + c % inner_c),
         )
+
+    @pl.when(jnp.logical_not(is_root))
+    def _():
+        pl.semaphore_wait(barrier, greeted + roots)
+        for root in range(roots):
+            to_root(root).start()
 
     load_now.wait()
     load_inflow.wait()
@@ -345,17 +335,9 @@
 
     @pl.when(is_root)
     def _():
-        pl.semaphore_wait(barrier, greeted + roots - 1 + stages[1][0] - 1 + stages[0][0] - 1)
-
-    @pl.when(jnp.logical_not(is_root))
-    def _():
-        pl.semaphore_wait(barrier, greeted + roots)
-
-    for root in range(roots):
-
-        @pl.when(plane != root)
-        def _(root=root):
-            to_root(root).start()
+        pl.semaphore_wait(barrier, greeted + roots - 1 + len(mates))
+        for root in range(roots):
+            pl.when(plane != root)(to_root(root).start)
 
     copies[3].start()
     pl.when(jnp.logical_not(answer_left))(copies[2].start)
@@ -364,6 +346,12 @@
 
     pl.when(jnp.logical_not(is_root))(at_home)
 
+    @pl.when(is_root)
+    def _():
+        rows[1] = arrived(slots_z, 0, rows[0])
+        for k, there in enumerate(mates):
+            send(rows.at[1], slots_p.at[k], stage_send.at[1], stage_recv.at[1], there).start()
+
     @pl.when(answer_below)
     def _():
         copies[1].wait_recv()
@@ -378,16 +366,6 @@
     def _():
         copies[3].wait_recv()
         copies[2].start()
-
-    @pl.when(is_root)
-    def _():
-        rows[1] = stage_end(2)
-        stage_start(1)
-
-    @pl.when(is_root)
-    def _():
-        rows[0] = stage_end(1)
-        stage_start(0)
 
     pl.when(jnp.logical_not(answer_below))(copies[1].wait_recv)
     pl.when(jnp.logical_not(answer_above))(copies[0].wait_recv)
@@ -471,10 +449,10 @@
 
     children = [
         send(
-            rows.at[3],
+            rows.at[2],
             told.at[0],
-            stage_send.at[3],
-            stage_recv.at[3],
+            stage_send.at[2],
+            stage_recv.at[2],
             (s, (c + k * inner_c) % size_c),
         )
         for k in range(1, planes - roots + 1)
@@ -482,9 +460,9 @@
 
     @pl.when(is_root)
     def _():
-        fastest = stage_end(0)
-        rows[3] = fastest
-        fast_ref[...] = fastest
+        fastest = arrived(slots_p, 1, rows[1])
+        rows[2] = fastest
+        step_ref[...] = 0.3 / fastest
 
     @pl.when(plane == roots - 1)
     def _():
@@ -494,36 +472,33 @@
     @pl.when(jnp.logical_not(is_root))
     def _():
         children[0].wait_recv()
-        fast_ref[...] = told[0]
+        step_ref[...] = 0.3 / told[0]
 
     for copy in copies:
         copy.wait_send()
 
-    def sent(count, stage):
-        span = slots2.at[pl.ds(0, count)]
-        send(span, span, stage_send.at[stage], stage_recv.at[stage], right).wait_send()
+    def sent(slots, stage):
+        send(slots, slots, stage_send.at[stage], stage_recv.at[stage], right).wait_send()
 
     @pl.when(is_root)
     def _():
-        for stage in range(2):
-            stage_total(stage).wait_send()
+        sent(slots_p, 1)
         if roots > 1:
-            sent(roots - 1, 2)
+            sent(slots_z.at[pl.ds(0, roots - 1)], 0)
 
     @pl.when(plane == roots - 1)
     def _():
-        sent(planes - roots, 3)
+        sent(slots_z.at[pl.ds(0, planes - roots)], 2)
 
     @pl.when(jnp.logical_not(is_root))
     def _():
-        sent(roots, 2)
+        sent(slots_z.at[pl.ds(0, roots)], 0)
 
 
 def shards(sizes, state_now, state_base, inflow):
     size = jnp.float32
-    n0, n1, n2 = (sizes[0], sizes[1] * sizes[2], sizes[3])
     inflow_t = jnp.transpose(inflow, (0, 3, 1, 2))
-    part, rate, fast = pl.pallas_call(
+    part, rate, step = pl.pallas_call(
         functools.partial(kernel, sizes),
         out_shape=(
             jax.ShapeDtypeStruct((7, 8, 8, 128), size),
@@ -545,16 +520,15 @@
             pltpu.VMEM((7, 8, 128), size),
             pltpu.VMEM((7, 8, 128), size),
             pltpu.VMEM((7, 8, 128), size),
-            pltpu.VMEM((4, 1, 128), size),
-            pltpu.VMEM((n0 - 1, 1, 128), size),
-            pltpu.VMEM((n1 - 1, 1, 128), size),
-            pltpu.VMEM((n2 - 1, 1, 128), size),
+            pltpu.VMEM((3, 1, 128), size),
+            pltpu.VMEM((sizes[3] - 1, 1, 128), size),
+            pltpu.VMEM((sizes[0] * sizes[1] * sizes[2] - 1, 1, 128), size),
             pltpu.VMEM((1, 1, 128), size),
             pltpu.SemaphoreType.DMA((3,)),
             pltpu.SemaphoreType.DMA((4,)),
             pltpu.SemaphoreType.DMA((4,)),
-            pltpu.SemaphoreType.DMA((4,)),
-            pltpu.SemaphoreType.DMA((4,)),
+            pltpu.SemaphoreType.DMA((3,)),
+            pltpu.SemaphoreType.DMA((3,)),
         ],
         compiler_params=pltpu.CompilerParams(
             collective_id=0, has_side_effects=True, vmem_limit_bytes=32 * 1024 * 1024
@@ -564,7 +538,7 @@
         pltpu.with_memory_space_constraint(state_base, pltpu.HBM),
         pltpu.with_memory_space_constraint(inflow_t, pltpu.HBM),
     )
-    return part + 0.3 / fast[0, 0] * rate.reshape(state_now.shape)
+    return part + step.reshape(1, 1, 1, 128) * rate.reshape(state_now.shape)
 
 
 def solution(mesh):

time: 31.2 us -> 29.2 us (0.936)
  Pallas kernels: 30.3 us -> 28.3 us
    pallas_call x1, Pallas kernels: 30.3 us -> 28.3 us  [shards(): pl.pallas_call(functools.partial(kernel, sizes), out_shape=(jax.ShapeDtyp...]
where the time goes in v6:
time: 29.2 us; the launch traced here: 29.1 us
  Pallas kernels  28.3 us (97%)
  other arithmetic  0.72 us (2%)
    pallas_call x1, Pallas kernels, shards(): pl.pallas_call(functools.partial(kernel, sizes), out_shape=(jax.ShapeDtyp...  28.3 us
    add x1, other arithmetic, shards(): return part + step.reshape(1, 1, 1, 128) * rate.reshape(state_now.shape)  0.72 us

profile of v6, /device:TPU:1, one launch (start us, length us, event | category | flops | bytes accessed | tf_op | source)
XLA Modules:
  0.0 29.1 jit_solution(8251370559482843251)
XLA Ops:
  0.0 28.3 %shard_map.37 = (f32[7,8,8,128]{3,2,1,0:T(8,128)S(1)}, f32[7,64,128]{2,1,0:T(8,128)S(1)}, f32[1,128]{1,0:T(1,128)S(1)}) custom-call(f32[7,8,8,128]{3,2,1,0:T(8,128)} %now_ref.1, f32[7,8,8,128]{3,2,1,0:T(8,128)} %base_ref.1, f32[7,3,8,8]{3,2,1,0:T(8,128)} %bitcast.7), custom_call_target="tpu_custom_call" | custom-call | tf_op jit(solution)/shard_map/pallas_call | solution.py:501
  28.3 0.7 %fusion = f32[7,8,8,128]{3,2,1,0:T(8,128)} fusion(f32[7,8,8,128]{3,2,1,0:T(8,128)S(1)} %get-tuple-element.8, f32[7,64,128]{2,1,0:T(8,128)S(1)} %get-tuple-element.10, f32[128]{0:T(128)S(1)} %bitcast.6), kind=kLoop, calls=%fused_computation.1 | loop fusion | flops 114688 | bytes 688640 | tf_op jit(solution)/shard_map/add | solution.py:541

commit v7 on v6

--- a/solution.py
+++ b/solution.py
@@ -197,16 +197,6 @@
     stage_send,
     stage_recv,
 ):
-    size_s, size_c = (sizes[0] * sizes[2], sizes[1] * sizes[3])
-    s, c = (lax.axis_index("stream"), lax.axis_index("cross"))
-    left, right = (((s + size_s - 1) % size_s, c), ((s + 1) % size_s, c))
-    below, above = ((s, (c + size_c - 1) % size_c), (s, (c + 1) % size_c))
-    mates, others = (in_plane(sizes), along_z(sizes))
-    inner_c, planes = (sizes[1], sizes[3])
-    roots = max(1, planes // 3)
-    plane = c // inner_c
-    is_root = plane < roots
-
     load_base = pltpu.make_async_copy(base_ref, base, in_sems.at[0])
     load_now = pltpu.make_async_copy(now_ref, now, in_sems.at[1])
     load_inflow = pltpu.make_async_copy(inflow_ref, inflow, in_sems.at[2])
@@ -214,6 +204,15 @@
     load_now.start()
     load_inflow.start()
 
+    size_s, size_c = (sizes[0] * sizes[2], sizes[1] * sizes[3])
+    s, c = (lax.axis_index("stream"), lax.axis_index("cross"))
+    left, right = (((s + size_s - 1) % size_s, c), ((s + 1) % size_s, c))
+    below, above = ((s, (c + size_c - 1) % size_c), (s, (c + 1) % size_c))
+    inner_c, planes = (sizes[1], sizes[3])
+    roots = max(1, planes // 3)
+    plane = c // inner_c
+    is_root = plane < roots
+
     barrier = pltpu.get_barrier_semaphore()
 
     def greet(there):
@@ -223,12 +222,12 @@
     first_c, last_c = (c % inner_c == 0, c % inner_c == inner_c - 1)
     flip = s // sizes[0] > 0
     answer_left = first_s
-    answer_above = last_c & flip
-    answer_below = first_c & jnp.logical_not(flip)
+    answer_above = last_c & flip & (plane != planes - 1)
+    answer_below = first_c & (jnp.logical_not(flip) | (plane == 0))
     greet(left)
     pl.when(jnp.logical_not(last_s))(lambda: greet(right))
-    pl.when(jnp.logical_not(first_c & flip))(lambda: greet(below))
-    pl.when(jnp.logical_not(last_c & jnp.logical_not(flip)))(lambda: greet(above))
+    pl.when(jnp.logical_not(first_c) | answer_below)(lambda: greet(below))
+    pl.when(jnp.logical_not(last_c) | answer_above)(lambda: greet(above))
     greeted = (
         1
         + jnp.where(answer_left, 0, 1)
@@ -238,7 +237,7 @@
 
     @pl.when(is_root)
     def _():
-        for there in others + mates:
+        for there in along_z(sizes) + in_plane(sizes):
             greet(there)
 
     now_rows = now.reshape(7, 64, 128)
@@ -335,7 +334,7 @@
 
     @pl.when(is_root)
     def _():
-        pl.semaphore_wait(barrier, greeted + roots - 1 + len(mates))
+        pl.semaphore_wait(barrier, greeted + roots - 1 + slots_p.shape[0])
         for root in range(roots):
             pl.when(plane != root)(to_root(root).start)
 
@@ -349,7 +348,7 @@
     @pl.when(is_root)
     def _():
         rows[1] = arrived(slots_z, 0, rows[0])
-        for k, there in enumerate(mates):
+        for k, there in enumerate(in_plane(sizes)):
             send(rows.at[1], slots_p.at[k], stage_send.at[1], stage_recv.at[1], there).start()
 
     @pl.when(answer_below)
@@ -458,6 +457,22 @@
         for k in range(1, planes - roots + 1)
     ]
 
+    for copy in copies:
+        copy.wait_send()
+
+    def sent(slots, stage):
+        send(slots, slots, stage_send.at[stage], stage_recv.at[stage], right).wait_send()
+
+    @pl.when(is_root)
+    def _():
+        sent(slots_p, 1)
+        if roots > 1:
+            sent(slots_z.at[pl.ds(0, roots - 1)], 0)
+
+    @pl.when(jnp.logical_not(is_root))
+    def _():
+        sent(slots_z.at[pl.ds(0, roots)], 0)
+
     @pl.when(is_root)
     def _():
         fastest = arrived(slots_p, 1, rows[1])
@@ -474,25 +489,9 @@
         children[0].wait_recv()
         step_ref[...] = 0.3 / told[0]
 
-    for copy in copies:
-        copy.wait_send()
-
-    def sent(slots, stage):
-        send(slots, slots, stage_send.at[stage], stage_recv.at[stage], right).wait_send()
-
-    @pl.when(is_root)
-    def _():
-        sent(slots_p, 1)
-        if roots > 1:
-            sent(slots_z.at[pl.ds(0, roots - 1)], 0)
-
     @pl.when(plane == roots - 1)
     def _():
         sent(slots_z.at[pl.ds(0, planes - roots)], 2)
-
-    @pl.when(jnp.logical_not(is_root))
-    def _():
-        sent(slots_z.at[pl.ds(0, roots)], 0)
 
 
 def shards(sizes, state_now, state_base, inflow):

time: 29.2 us -> 29 us (level)
  no operation moved by 1% of the time
where the time goes in v7:
time: 29 us; the launch traced here: 28.9 us
  Pallas kernels  28.1 us (97%)
  other arithmetic  0.72 us (2%)
    pallas_call x1, Pallas kernels, shards(): pl.pallas_call(functools.partial(kernel, sizes), out_shape=(jax.ShapeDtyp...  28.1 us
    add x1, other arithmetic, shards(): return part + step.reshape(1, 1, 1, 128) * rate.reshape(state_now.shape)  0.72 us

profile of v7, /device:TPU:1, one launch (start us, length us, event | category | flops | bytes accessed | tf_op | source)
XLA Modules:
  0.0 28.9 jit_solution(11104134660837813951)
XLA Ops:
  0.0 28.1 %shard_map.37 = (f32[7,8,8,128]{3,2,1,0:T(8,128)S(1)}, f32[7,64,128]{2,1,0:T(8,128)S(1)}, f32[1,128]{1,0:T(1,128)S(1)}) custom-call(f32[7,8,8,128]{3,2,1,0:T(8,128)} %now_ref.1, f32[7,8,8,128]{3,2,1,0:T(8,128)} %base_ref.1, f32[7,3,8,8]{3,2,1,0:T(8,128)} %bitcast.7), custom_call_target="tpu_custom_call" | custom-call | tf_op jit(solution)/shard_map/pallas_call | solution.py:500
  28.1 0.7 %fusion = f32[7,8,8,128]{3,2,1,0:T(8,128)} fusion(f32[7,8,8,128]{3,2,1,0:T(8,128)S(1)} %get-tuple-element.8, f32[7,64,128]{2,1,0:T(8,128)S(1)} %get-tuple-element.10, f32[128]{0:T(128)S(1)} %bitcast.6), kind=kLoop, calls=%fused_computation.1 | loop fusion | flops 114688 | bytes 688640 | tf_op jit(solution)/shard_map/add | solution.py:540

commit v8 on v7

--- a/solution.py
+++ b/solution.py
@@ -149,11 +149,15 @@
     return there
 
 
+def core_mate(s):
+    return s // 2 * 2 + 1 - s % 2
+
+
 def along_z(sizes):
     _, inner_c, _, planes = sizes
     s, c = (lax.axis_index("stream"), lax.axis_index("cross"))
     offsets = sorted(range(1, planes), key=lambda k: -min(k, planes - k))
-    return [(s, (c + k * inner_c) % (planes * inner_c)) for k in offsets]
+    return [(core_mate(s), (c + k * inner_c) % (planes * inner_c)) for k in offsets]
 
 
 def send(source, target, send_sem, recv_sem, to):
@@ -222,14 +226,15 @@
     first_c, last_c = (c % inner_c == 0, c % inner_c == inner_c - 1)
     flip = s // sizes[0] > 0
     answer_left = first_s
+    leftmost, rightmost = (s == 0, s == size_s - 1)
     answer_above = last_c & flip & (plane != planes - 1)
     answer_below = first_c & (jnp.logical_not(flip) | (plane == 0))
-    greet(left)
-    pl.when(jnp.logical_not(last_s))(lambda: greet(right))
     pl.when(jnp.logical_not(first_c) | answer_below)(lambda: greet(below))
     pl.when(jnp.logical_not(last_c) | answer_above)(lambda: greet(above))
+    pl.when(s > 0)(lambda: greet(left))
+    pl.when(jnp.logical_not(last_s))(lambda: greet(right))
     greeted = (
-        1
+        jnp.where(s < size_s - 1, 1, 0)
         + jnp.where(answer_left, 0, 1)
         + jnp.where(answer_above, 0, 1)
         + jnp.where(answer_below, 0, 1)
@@ -262,9 +267,11 @@
     rows[0] = jnp.broadcast_to(jnp.max(most, keepdims=True), (1, 128))
     def arrived(slots, stage, own):
         send(slots, slots, stage_send.at[stage], stage_recv.at[stage], right).wait_recv()
-        for k in range(slots.shape[0]):
-            own = jnp.maximum(own, slots[k])
-        return own
+        values = [own] + [slots[k] for k in range(slots.shape[0])]
+        while len(values) > 1:
+            pairs = [jnp.maximum(*values[k : k + 2]) for k in range(0, len(values) - 1, 2)]
+            values = pairs + values[2 * len(pairs) :]
+        return values[0]
 
     def to_root(root):
         return send(
@@ -272,7 +279,7 @@
             slots_z.at[(root - plane + planes) % planes - 1],
             stage_send.at[0],
             stage_recv.at[0],
-            (s, root * inner_c + c % inner_c),
+            (core_mate(s), root * inner_c + c % inner_c),
         )
 
     @pl.when(jnp.logical_not(is_root))
@@ -338,7 +345,7 @@
         for root in range(roots):
             pl.when(plane != root)(to_root(root).start)
 
-    copies[3].start()
+    pl.when(jnp.logical_not(rightmost))(copies[3].start)
     pl.when(jnp.logical_not(answer_left))(copies[2].start)
     pl.when(jnp.logical_not(answer_above))(copies[1].start)
     pl.when(jnp.logical_not(answer_below))(copies[0].start)
@@ -361,7 +368,7 @@
         copies[0].wait_recv()
         copies[1].start()
 
-    @pl.when(answer_left)
+    @pl.when(answer_left & jnp.logical_not(leftmost))
     def _():
         copies[3].wait_recv()
         copies[2].start()
@@ -409,7 +416,7 @@
 
     lax.fori_loop(0, 9, face, 0)
 
-    copies[2].wait_recv()
+    pl.when(jnp.logical_not(rightmost))(copies[2].wait_recv)
     pl.when(jnp.logical_not(answer_left))(copies[3].wait_recv)
 
     @pl.when(s == 0)
@@ -452,13 +459,15 @@
             told.at[0],
             stage_send.at[2],
             stage_recv.at[2],
-            (s, (c + k * inner_c) % size_c),
+            (core_mate(s), (c + k * inner_c) % size_c),
         )
         for k in range(1, planes - roots + 1)
     ]
 
-    for copy in copies:
-        copy.wait_send()
+    copies[0].wait_send()
+    copies[1].wait_send()
+    pl.when(jnp.logical_not(leftmost))(copies[2].wait_send)
+    pl.when(jnp.logical_not(rightmost))(copies[3].wait_send)
 
     def sent(slots, stage):
         send(slots, slots, stage_send.at[stage], stage_recv.at[stage], right).wait_send()

time: 29 us -> 28.6 us (0.986)
  Pallas kernels: 28.1 us -> 27.8 us
    pallas_call x1, Pallas kernels: 28.1 us -> 27.8 us  [shards(): pl.pallas_call(functools.partial(kernel, sizes), out_shape=(jax.ShapeDtyp...]
where the time goes in v8:
time: 28.6 us; the launch traced here: 28.5 us
  Pallas kernels  27.8 us (97%)
  other arithmetic  0.72 us (3%)
    pallas_call x1, Pallas kernels, shards(): pl.pallas_call(functools.partial(kernel, sizes), out_shape=(jax.ShapeDtyp...  27.8 us
    add x1, other arithmetic, shards(): return part + step.reshape(1, 1, 1, 128) * rate.reshape(state_now.shape)  0.72 us

profile of v8, /device:TPU:1, one launch (start us, length us, event | category | flops | bytes accessed | tf_op | source)
XLA Modules:
  0.0 28.5 jit_solution(18029292666887369113)
XLA Ops:
  0.0 27.8 %shard_map.37 = (f32[7,8,8,128]{3,2,1,0:T(8,128)S(1)}, f32[7,64,128]{2,1,0:T(8,128)S(1)}, f32[1,128]{1,0:T(1,128)S(1)}) custom-call(f32[7,8,8,128]{3,2,1,0:T(8,128)} %now_ref.1, f32[7,8,8,128]{3,2,1,0:T(8,128)} %base_ref.1, f32[7,3,8,8]{3,2,1,0:T(8,128)} %bitcast.7), custom_call_target="tpu_custom_call" | custom-call | tf_op jit(solution)/shard_map/pallas_call | solution.py:509
  27.8 0.7 %fusion = f32[7,8,8,128]{3,2,1,0:T(8,128)} fusion(f32[7,8,8,128]{3,2,1,0:T(8,128)S(1)} %get-tuple-element.8, f32[7,64,128]{2,1,0:T(8,128)S(1)} %get-tuple-element.10, f32[128]{0:T(128)S(1)} %bitcast.6), kind=kLoop, calls=%fused_computation.1 | loop fusion | flops 114688 | bytes 688640 | tf_op jit(solution)/shard_map/add | solution.py:549

commit v9 on v8

--- a/solution.py
+++ b/solution.py
@@ -135,7 +135,7 @@
 
     def distance(offset):
         i, j = offset
-        return min(i, inner_s - i) / 2 + min(j, length - j)
+        return (min(i, inner_s - i) + 1) // 2 + min(j, length - j)
 
     there = []
     for i, j in sorted(offsets, key=lambda offset: -distance(offset)):

time: 28.6 us -> 28.5 us (level)
  no operation moved by 1% of the time
where the time goes in v9:
time: 28.5 us; the launch traced here: 28.4 us
  Pallas kernels  27.7 us (97%)
  other arithmetic  0.72 us (3%)
    pallas_call x1, Pallas kernels, shards(): pl.pallas_call(functools.partial(kernel, sizes), out_shape=(jax.ShapeDtyp...  27.7 us
    add x1, other arithmetic, shards(): return part + step.reshape(1, 1, 1, 128) * rate.reshape(state_now.shape)  0.72 us

profile of v9, /device:TPU:1, one launch (start us, length us, event | category | flops | bytes accessed | tf_op | source)
XLA Modules:
  0.0 28.4 jit_solution(8479500545327308672)
XLA Ops:
  0.0 27.7 %shard_map.37 = (f32[7,8,8,128]{3,2,1,0:T(8,128)S(1)}, f32[7,64,128]{2,1,0:T(8,128)S(1)}, f32[1,128]{1,0:T(1,128)S(1)}) custom-call(f32[7,8,8,128]{3,2,1,0:T(8,128)} %now_ref.1, f32[7,8,8,128]{3,2,1,0:T(8,128)} %base_ref.1, f32[7,3,8,8]{3,2,1,0:T(8,128)} %bitcast.7), custom_call_target="tpu_custom_call" | custom-call | tf_op jit(solution)/shard_map/pallas_call | solution.py:509
  27.7 0.7 %fusion = f32[7,8,8,128]{3,2,1,0:T(8,128)} fusion(f32[7,8,8,128]{3,2,1,0:T(8,128)S(1)} %get-tuple-element.8, f32[7,64,128]{2,1,0:T(8,128)S(1)} %get-tuple-element.10, f32[128]{0:T(128)S(1)} %bitcast.6), kind=kLoop, calls=%fused_computation.1 | loop fusion | flops 114688 | bytes 688640 | tf_op jit(solution)/shard_map/add | solution.py:549

commit v10 on v9

--- a/solution.py
+++ b/solution.py
@@ -205,8 +205,6 @@
     load_now = pltpu.make_async_copy(now_ref, now, in_sems.at[1])
     load_inflow = pltpu.make_async_copy(inflow_ref, inflow, in_sems.at[2])
     load_base.start()
-    load_now.start()
-    load_inflow.start()
 
     size_s, size_c = (sizes[0] * sizes[2], sizes[1] * sizes[3])
     s, c = (lax.axis_index("stream"), lax.axis_index("cross"))
@@ -261,6 +259,8 @@
         return jnp.maximum(most, swift + sound(w[0] + w[1], w[5], gamma, stiff))
 
     load_base.wait()
+    load_now.start()
+    load_inflow.start()
     most = jnp.zeros((8, 128), jnp.float32)
     for y in range(8):
         most = speed(y, most)

time: 28.5 us -> 28.6 us (level)
  no operation moved by 1% of the time
where the time goes in v10:
time: 28.6 us; the launch traced here: 28.4 us
  Pallas kernels  27.7 us (97%)
  other arithmetic  0.72 us (3%)
    pallas_call x1, Pallas kernels, shards(): pl.pallas_call(functools.partial(kernel, sizes), out_shape=(jax.ShapeDtyp...  27.7 us
    add x1, other arithmetic, shards(): return part + step.reshape(1, 1, 1, 128) * rate.reshape(state_now.shape)  0.72 us

profile of v10, /device:TPU:1, one launch (start us, length us, event | category | flops | bytes accessed | tf_op | source)
XLA Modules:
  0.0 28.4 jit_solution(3064990187841182927)
XLA Ops:
  0.0 27.7 %shard_map.37 = (f32[7,8,8,128]{3,2,1,0:T(8,128)S(1)}, f32[7,64,128]{2,1,0:T(8,128)S(1)}, f32[1,128]{1,0:T(1,128)S(1)}) custom-call(f32[7,8,8,128]{3,2,1,0:T(8,128)} %now_ref.1, f32[7,8,8,128]{3,2,1,0:T(8,128)} %base_ref.1, f32[7,3,8,8]{3,2,1,0:T(8,128)} %bitcast.7), custom_call_target="tpu_custom_call" | custom-call | tf_op jit(solution)/shard_map/pallas_call | solution.py:509
  27.7 0.7 %fusion = f32[7,8,8,128]{3,2,1,0:T(8,128)} fusion(f32[7,8,8,128]{3,2,1,0:T(8,128)S(1)} %get-tuple-element.8, f32[7,64,128]{2,1,0:T(8,128)S(1)} %get-tuple-element.10, f32[128]{0:T(128)S(1)} %bitcast.6), kind=kLoop, calls=%fused_computation.1 | loop fusion | flops 114688 | bytes 688640 | tf_op jit(solution)/shard_map/add | solution.py:549

commit v11 on v10

--- a/solution.py
+++ b/solution.py
@@ -211,7 +211,7 @@
     left, right = (((s + size_s - 1) % size_s, c), ((s + 1) % size_s, c))
     below, above = ((s, (c + size_c - 1) % size_c), (s, (c + 1) % size_c))
     inner_c, planes = (sizes[1], sizes[3])
-    roots = max(1, planes // 3)
+    roots = max(1, planes // 4)
     plane = c // inner_c
     is_root = plane < roots
 

time: 28.6 us -> 28.6 us (level)
  no operation moved by 1% of the time
where the time goes in v11:
time: 28.6 us; the launch traced here: 28.4 us
  Pallas kernels  27.7 us (97%)
  other arithmetic  0.72 us (3%)
    pallas_call x1, Pallas kernels, shards(): pl.pallas_call(functools.partial(kernel, sizes), out_shape=(jax.ShapeDtyp...  27.7 us
    add x1, other arithmetic, shards(): return part + step.reshape(1, 1, 1, 128) * rate.reshape(state_now.shape)  0.72 us

profile of v11, /device:TPU:1, one launch (start us, length us, event | category | flops | bytes accessed | tf_op | source)
XLA Modules:
  0.0 28.4 jit_solution(12154970885806339328)
XLA Ops:
  0.0 27.7 %shard_map.37 = (f32[7,8,8,128]{3,2,1,0:T(8,128)S(1)}, f32[7,64,128]{2,1,0:T(8,128)S(1)}, f32[1,128]{1,0:T(1,128)S(1)}) custom-call(f32[7,8,8,128]{3,2,1,0:T(8,128)} %now_ref.1, f32[7,8,8,128]{3,2,1,0:T(8,128)} %base_ref.1, f32[7,3,8,8]{3,2,1,0:T(8,128)} %bitcast.7), custom_call_target="tpu_custom_call" | custom-call | tf_op jit(solution)/shard_map/pallas_call | solution.py:509
  27.7 0.7 %fusion = f32[7,8,8,128]{3,2,1,0:T(8,128)} fusion(f32[7,8,8,128]{3,2,1,0:T(8,128)S(1)} %get-tuple-element.8, f32[7,64,128]{2,1,0:T(8,128)S(1)} %get-tuple-element.10, f32[128]{0:T(128)S(1)} %bitcast.6), kind=kLoop, calls=%fused_computation.1 | loop fusion | flops 114688 | bytes 688640 | tf_op jit(solution)/shard_map/add | solution.py:549
